TPU v7x, 256 devices: a whole 4x4x8 slice. The times are simulated.
256 devices in a mesh: freq: 8 (over x, y_lo), bond: 32 (over z, y_hi, core).
Axes of the slice: x: 4, y: 4 (y_hi: 2, y_lo: 2; y = y_hi * 2 + y_lo), z: 8, core: 2. Of those that a mesh axis runs over, the one named last changes fastest.
Arguments:
- gamma: bfloat16 [2, 16, 128, 384, 384], P(None, 'freq', 'bond'), may hold values from -1 to 1
- green: float32 [2, 16, 128, 256], P(None, 'freq', 'bond'), may hold values from -6 to 6
- single: float32 [2, 16, 128, 256], P(None, 'freq', 'bond'), may hold values from -6 to 6
- bond_site: int32 [384], replicated, may hold values from 0 to 255
- causal_mask: int32 [16, 3, 3], P('freq'), may hold values 0 or 1
- site_perm: int32 [384], replicated, may hold values from 0 to 383, each once
Outputs:
- p_vertex: bfloat16 [2, 16, 384, 128, 384], P(None, 'freq', 'bond')
Inputs may be any that keep to these rules, and one draw needn't show every extreme that they name: `bond_site`: each of the 384 bond-Keldysh indices names one site. `causal_mask`: 1 keeps a causality block of 128 x 128 entries, 0 removes it. `site_perm`: a permutation of the 384 column indices.
All inputs are finite; a program needn't handle non-finite values.
Results may differ from a plain program's by a relative error of at most 0.0049.
Values may be sent and summed in bfloat16 or wider, within the bound.
No kernel may reach another device: no remote copies, remote signals or barrier semaphores. Data moves between devices by JAX's collectives and lax.ppermute only.
A program may use at most 128 MiB of HBM per device.

v0:
```python
import math

import jax
import jax.numpy as jnp
from jax import lax
from jax.sharding import PartitionSpec as P


def side_by_side(arrays, axis, dim, along):
    both = jnp.concatenate(arrays, axis=along)
    out, at, finished = (lax.all_gather(both, axis, axis=dim, tiled=True), 0, [])
    for a in arrays:
        finished.append(lax.slice_in_dim(out, at, at + a.shape[along], axis=along))
        at += a.shape[along]
    return tuple(finished)


def times_complex(first_real, first_imag, second_real, second_imag):
    return (
        first_real * second_real - first_imag * second_imag,
        first_real * second_imag + first_imag * second_real,
    )


def products(pattern, left, right):
    return jnp.einsum(pattern, left, right, preferred_element_type=jnp.float32)


def complex_flow(pattern, left_real, left_imag, gamma_real, gamma_imag):
    flow_real = products(pattern, left_real, gamma_real) - products(pattern, left_imag, gamma_imag)
    flow_imag = products(pattern, left_real, gamma_imag) + products(pattern, left_imag, gamma_real)
    return (flow_real, flow_imag)


def compute_flows(gamma_part, bubble_part, mask_part, site_perm):
    order = gamma_part.shape[-1]
    blocks = mask_part.shape[-1]
    width = order // blocks
    gamma_real = gamma_part[0].astype(jnp.float32)
    gamma_imag = gamma_part[1].astype(jnp.float32)
    bubble_real = bubble_part[0][:, :, None, :]
    bubble_imag = bubble_part[1][:, :, None, :]
    left_real = (gamma_real * bubble_real - gamma_imag * bubble_imag).astype(jnp.bfloat16)
    left_imag = (gamma_real * bubble_imag + gamma_imag * bubble_real).astype(jnp.bfloat16)
    flow_real, flow_imag = complex_flow(
        "wsrk,wskc->wrsc", left_real, left_imag, gamma_part[0], gamma_part[1]
    )
    spread = jnp.repeat(jnp.repeat(mask_part, width, axis=1), width, axis=2).astype(jnp.float32)
    flow_real = flow_real * spread[:, :, None, :]
    flow_imag = flow_imag * spread[:, :, None, :]
    rounded = jnp.stack([flow_real, flow_imag]).astype(jnp.bfloat16)
    return jnp.take(rounded, site_perm, axis=4)


def body(gamma, green, single, bond_site, causal_mask, site_perm):
    local = green.shape[1]
    count = local * lax.axis_size("freq")
    whole_green, whole_single = side_by_side((green, single), "freq", 1, 0)
    green_bond = jnp.take(whole_green, bond_site, axis=3)
    single_bond = jnp.take(whole_single, bond_site, axis=3)
    owned = lax.axis_index("freq") * local + jnp.arange(local, dtype=jnp.int32)
    shifts = (jnp.arange(count, dtype=jnp.int32)[None, :] + owned[:, None]) % count
    green_moved = jnp.take(green_bond, shifts, axis=1)
    single_moved = jnp.take(single_bond, shifts, axis=1)
    first = times_complex(
        green_bond[0][None], green_bond[1][None], single_moved[0], single_moved[1]
    )
    second = times_complex(
        single_bond[0][None], single_bond[1][None], green_moved[0], green_moved[1]
    )
    factor = 1.0 / math.sqrt(count)
    bubble = jnp.stack(
        [
            jnp.sum(first[0] + second[0], axis=1) * factor,
            jnp.sum(first[1] + second[1], axis=1) * factor,
        ]
    )
    flows = compute_flows(gamma, bubble, causal_mask, site_perm)
    return lax.all_to_all(flows, "bond", split_axis=2, concat_axis=3, tiled=True)


def solution(mesh):
    in_specs = (
        P(None, "freq", "bond", None, None),
        P(None, "freq", "bond", None),
        P(None, "freq", "bond", None),
        P(),
        P("freq", None, None),
        P(),
    )
    out_specs = P(None, "freq", "bond", None, None)
    return jax.shard_map(body, mesh=mesh, in_specs=in_specs, out_specs=out_specs, check_vma=False)
```

profile of v0, /device:TPU:1, one launch (start us, length us, event | category | flops | bytes accessed | tf_op | source)
XLA Modules:
  0.0 257.3 jit_solution(2193904891974347826)
XLA Ops:
  1.5 0.7 pad_maximum_fusion.1
  2.3 23.4 %all_gather.3 = f32[4,16,4,256]{3,2,0,1:T(4,128)S(1)} all-gather(f32[4,2,4,256]{3,2,0,1:T(4,128)S(1)} %copy.78), channel_id=1, replica_groups=mesh['freq'=8,'bond'=32] {'freq'}, dimensions={1}, use_global_device_ids=true | all-gather | bytes 294912 | tf_op jit(solution)/shard_map/all_gather | solution.py:11
  26.5 3.1 %gather_fusion.1 = f32[384,2,16,4]{2,3,1,0:T(4,128)} fusion(f32[2,16,4,256]{1,2,3,0:T(4,128)S(1)} %copy.79, s32[1024]{0:T(1024)S(1)} %pad_clamp_fusion.2), kind=kCustom, calls=%fused_computation.clone | custom fusion | bytes 394752 | tf_op jit(solution)/shard_map/jit(_take)/gather | solution.py:59
  29.6 3.1 %gather_fusion.2 = f32[384,2,16,4]{2,3,1,0:T(4,128)} fusion(f32[2,16,4,256]{1,2,3,0:T(4,128)S(1)} %copy.81, s32[1024]{0:T(1024)S(1)} %pad_clamp_fusion.2), kind=kCustom, calls=%fused_computation.2.clone | custom fusion | bytes 394752 | tf_op jit(solution)/shard_map/jit(_take)/gather | solution.py:60
  32.8 2.8 %select_bitcast_fusion.2 = (f32[2,16,4,384]{1,2,0,3:T(4,128)S(1)}, f32[2,16,4,384]{1,2,0,3:T(4,128)S(1)}) fusion(f32[384,2,16,4]{2,3,1,0:T(4,128)} %gather_fusion.1, pred[384]{0:T(512)(128)(4,1)S(1)} %compare_and_fusion.1, f32[384,2,16,4]{2,3,1,0:T(4,128)} %gather_fusion.2), kind=kLoop, calls=%fused_computation.40 | loop fusion | flops 98304 | bytes 786816 | tf_op jit(solution)/shard_map/jit(_take)/select_n | solution.py:59
  35.6 0.8 copy.86
  36.4 1.0 copy.82
  37.4 1.9 slice_bitcast_fusion.1
  39.5 0.8 gather_fusion.4
  40.4 0.8 gather_fusion.3
  41.3 1.4 copy.80
  42.6 1.4 copy.84
  44.9 7.0 %fusion.6 = f32[2,4,384,384]{3,2,1,0:T(8,128)} fusion(f32[2,4,384]{2,1,0:T(4,128)S(1)} %copy_multiply_fusion, f32[2,4,384]{2,1,0:T(4,128)S(1)} %copy_multiply_fusion.1, bf16[2,2,4,384,384]{4,3,2,1,0:T(8,128)(2,1)} %param.10), kind=kOutput, calls=%fused_computation.18 | convolution fusion | flops 913047552 | bytes 11821056 | tf_op jit(solution)/shard_map/wsrk,wskc->wrsc/dot_general | solution.py:26
  51.9 3.8 %fusion.4 = f32[2,4,384,384]{3,2,1,0:T(8,128)} fusion(f32[2,4,384]{2,1,0:T(4,128)S(1)} %copy_multiply_fusion, f32[2,4,384]{2,1,0:T(4,128)S(1)} %copy_multiply_fusion.1, bf16[2,2,4,384,384]{4,3,2,1,0:T(8,128)(2,1)S(1)} %bitcast.111), kind=kOutput, calls=%fused_computation.17 | convolution fusion | flops 913047552 | bytes 11821056 | tf_op jit(solution)/shard_map/wsrk,wskc->wrsc/dot_general | solution.py:26
  56.4 6.1 %fusion.12 = bf16[1,2,384,4,384]{4,2,3,1,0:T(8,128)(2,1)S(1)} fusion(f32[2,4,384,384]{3,2,1,0:T(8,128)} %fusion.6, f32[2,384,384]{2,1,0:T(8,128)S(1)} %copy.93, f32[2,4,384]{2,1,0:T(4,128)S(1)} %copy_multiply_fusion, f32[2,4,384]{2,1,0:T(4,128)S(1)} %copy_multiply_fusion.1, bf16[2,2,4,384,384]{4,3,2,1,0:T(8,128)(2,1)} %param.10), kind=kOutput, calls=%fused_computation.21 | convolution fusion | flops 916586496 | bytes 15360000 | tf_op jit(solution)/shard_map/wsrk,wskc->wrsc/dot_general | solution.py:26
  62.5 6.1 %fusion.13 = bf16[1,2,384,4,384]{4,2,3,1,0:T(8,128)(2,1)S(1)} fusion(f32[2,4,384,384]{3,2,1,0:T(8,128)} %fusion.4, f32[2,384,384]{2,1,0:T(8,128)S(1)} %copy.93, f32[2,4,384]{2,1,0:T(4,128)S(1)} %copy_multiply_fusion, f32[2,4,384]{2,1,0:T(4,128)S(1)} %copy_multiply_fusion.1, bf16[2,2,4,384,384]{4,3,2,1,0:T(8,128)(2,1)} %param.10), kind=kOutput, calls=%fused_computation.22 | convolution fusion | flops 916586496 | bytes 15360000 | tf_op jit(solution)/shard_map/wsrk,wskc->wrsc/dot_general | solution.py:26
  68.6 2.7 %pad_maximum_fusion = bf16[2,2,384,4,384]{4,2,3,1,0:T(8,128)(2,1)} fusion(bf16[1,2,384,4,384]{4,2,3,1,0:T(8,128)(2,1)S(1)} %fusion.13, bf16[1,2,384,4,384]{4,2,3,1,0:T(8,128)(2,1)S(1)} %fusion.12), kind=kLoop, calls=%fused_computation.13 | loop fusion | flops 2359296 | bytes 9437184 | tf_op jit(solution)/shard_map/stack | solution.py:51
  71.3 8.4 %copy.94 = bf16[2,2,384,4,384]{2,3,4,1,0:T(4,128)(2,1)} copy(bf16[2,2,384,4,384]{4,2,3,1,0:T(8,128)(2,1)} %pad_maximum_fusion) | data formatting | bytes 9437184 | tf_op jit(solution)/shard_map/stack | solution.py:51
  79.8 20.7 %gather_fusion = bf16[384,2,2,384,4]{3,4,2,1,0:T(4,128)(2,1)} fusion(bf16[2,2,384,4,384]{2,3,4,1,0:T(4,128)(2,1)} %copy.94, s32[1024]{0:T(1024)S(1)} %pad_clamp_fusion), kind=kCustom, calls=%fused_computation.4 | custom fusion | bytes 9438720 | tf_op jit(solution)/shard_map/jit(_take)/gather | solution.py:52
  100.5 6.8 %select_bitcast_fusion = bf16[2,2,384,4,384]{2,3,1,0,4:T(4,128)(2,1)} fusion(bf16[384,2,2,384,4]{3,4,2,1,0:T(4,128)(2,1)} %gather_fusion, pred[384]{0:T(512)(128)(4,1)S(1)} %compare_and_fusion.2), kind=kLoop, calls=%fused_computation.14 | loop fusion | flops 2359296 | bytes 9437568 | tf_op jit(solution)/shard_map/jit(_take)/select_n | solution.py:52
  107.3 10.3 %copy.95 = bf16[2,2,384,4,384]{4,3,1,0,2:T(4,128)(2,1)} copy(bf16[2,2,384,4,384]{2,3,1,0,4:T(4,128)(2,1)} %select_bitcast_fusion) | data formatting | bytes 9437184 | tf_op jit(solution)/shard_map/jit(_take)/select_n | solution.py:52
  117.6 124.8 %all_to_all.18 = bf16[2,2,384,4,384]{4,3,1,0,2:T(4,128)(2,1)} all-to-all(bf16[2,2,384,4,384]{4,3,1,0,2:T(4,128)(2,1)} %copy.95), channel_id=1, replica_groups=mesh['freq'=8,'bond'=32] {'bond'}, dimensions={2} | all-to-all | bytes 9437184 | tf_op jit(solution)/shard_map/all_to_all | solution.py:79
  242.3 9.4 %copy.97 = bf16[2,2,12,32,4,384]{5,1,4,3,2,0:T(2,128)(2,1)} copy(bf16[2,2,12,32,4,384]{5,4,1,0,2,3:T(4,128)(2,1)} %bitcast.105) | data formatting | bytes 9437184 | tf_op jit(solution)/shard_map/all_to_all | solution.py:79
  251.7 5.6 %copy.98 = bf16[2,2,12,128,384]{4,3,2,1,0:T(8,128)(2,1)} copy(bf16[2,2,12,128,384]{4,1,3,2,0:T(2,128)(2,1)} %bitcast.106) | data formatting | bytes 9437184 | tf_op jit(solution)/shard_map/all_to_all | solution.py:79
  (43 shorter events, 4.2 us)
Async XLA Ops:
  39.4 4.6 %copy-start.1 = (f32[16,4,384]{0,1,2:T(4,128)S(1)}, f32[16,4,384]{0,1,2:T(4,128)}, u32[]{:S(2)}) copy-start(f32[16,4,384]{0,1,2:T(4,128)} %get-tuple-element.11) | copy-start | bytes 294916
  39.4 4.9 %copy-start = (f32[16,4,384]{0,1,2:T(4,128)S(1)}, f32[16,4,384]{0,1,2:T(4,128)}, u32[]{:S(2)}) copy-start(f32[16,4,384]{0,1,2:T(4,128)} %get-tuple-element.12) | copy-start | bytes 294916
  44.7 7.2 %slice-start = ((s8[4718592]{0:T(1024)(128)(4,1)}), s8[4194304]{0:T(1024)(128)(4,1)S(1)}, s32[]{:S(2)}) async-start(s8[4718592]{0:T(1024)(128)(4,1)} %bitcast.110), calls=%async_computation.1 | async-start | bytes 8388608
  44.9 7.0 %slice-start.1 = ((s8[4718592]{0:T(1024)(128)(4,1)}), s8[524288]{0:T(1024)(128)(4,1)S(1)}, s32[]{:S(2)}) async-start(s8[4718592]{0:T(1024)(128)(4,1)} %bitcast.110), calls=%async_computation.2 | async-start | bytes 1048576
  51.9 3.8 %copy-start.2 = (s32[384]{0:T(512)S(1)}, s32[384]{0:T(512)}, u32[]{:S(2)}) copy-start(s32[384]{0:T(512)} %param.15) | copy-start | bytes 4612
  51.9 3.8 %copy-start.3 = (s32[2,3,3]{2,0,1:T(2,128)S(1)}, s32[2,3,3]{2,0,1:T(2,128)}, u32[]{:S(2)}) copy-start(s32[2,3,3]{2,0,1:T(2,128)} %param.14) | copy-start | bytes 220
where the time goes:
time: 258 us; the launch traced here: 257 us
  blocking collectives  148 us (57%)
  local copies, waits for them, and re-layouts  71 us (28%)
  matrix products  23 us (9%)
  other arithmetic  15 us (6%)
    all_to_all x1, blocking collectives, body(): lax.all_to_all(flows, 'bond', split_axis=2, concat_axis=3, tiled=True)  125 us
    all_gather x1, blocking collectives, side_by_side(): lax.all_gather(both, axis, axis=dim, tiled=True)  23.4 us
    dot_general x4, matrix products, products(): return jnp.einsum(pattern, left, right, preferred_element_type=jnp.float32)  23 us
    gather x1, local copies, waits for them, and re-layouts, compute_flows(): return jnp.take(rounded, site_perm, axis=4)  20.7 us
    all_to_all x2, local copies, waits for them, and re-layouts, body(): lax.all_to_all(flows, 'bond', split_axis=2, concat_axis=3, tiled=True)  15 us
    select_n x1, local copies, waits for them, and re-layouts, compute_flows(): return jnp.take(rounded, site_perm, axis=4)  10.3 us
    another operation x1, local copies, waits for them, and re-layouts, compute_flows(): rounded = jnp.stack([flow_real, flow_imag]).astype(jnp.bfloat16)  8.43 us
    select_n x2, other arithmetic, compute_flows(): return jnp.take(rounded, site_perm, axis=4)  6.84 us

commit v1 on v0

v1 whole, which is shorter than its diff:
```python
import functools
import math

import jax
import jax.numpy as jnp
from jax import lax
from jax.experimental import pallas as pl
from jax.experimental.pallas import tpu as pltpu
from jax.sharding import PartitionSpec as P


LANES = 128
PLANE = 4
FIRST = (3, 5)
REST = (4, 2, 6, 0, 1, 7)
GROUPS = ((3, 5), (4,), (2, 6), (0, 1), (7,))
VMEM = pl.BlockSpec(memory_space=pltpu.VMEM)
SMEM = pl.BlockSpec(memory_space=pltpu.SMEM)


def params(mib=24):
    return pltpu.CompilerParams(vmem_limit_bytes=mib * 1024 * 1024)


def spread_kernel(at, perm_ref, gamma_ref, copy_ref, out_ref, sems):
    count, order = out_ref.shape[1:3]
    copies = [
        pltpu.make_async_copy(gamma_ref.at[:, pl.ds(at + i, 1)], copy_ref.at[:, pl.ds(i, 1)], sems.at[i])
        for i in range(count)
    ]
    for copy in copies:
        copy.start()
    rows = lax.broadcasted_iota(jnp.int32, (order, order), 0)
    hot = (rows == perm_ref[...]).astype(jnp.float32).astype(jnp.bfloat16)
    for i in range(count):
        copies[i].wait()
        both = copy_ref[:, i].reshape(2 * order, order)
        both = jnp.dot(both, hot, preferred_element_type=jnp.float32).astype(jnp.bfloat16)
        out_ref[:, i] = both.reshape(2, order, order)


def spread(gamma, perm, half):
    _, count, order, _ = gamma.shape
    shape = jax.ShapeDtypeStruct((2, count // 2, order, order), jnp.bfloat16)
    return pl.pallas_call(
        functools.partial(spread_kernel, half * (count // 2)),
        in_specs=[VMEM, pl.BlockSpec(memory_space=pltpu.HBM)],
        out_specs=[VMEM, VMEM],
        out_shape=[shape, shape],
        scratch_shapes=[pltpu.SemaphoreType.DMA((count // 2,))],
        compiler_params=params(48),
        name="spread",
    )(perm, gamma)


def bubble_kernel(pos_ref, mine_ref, other_ref, site_ref, out_ref, all_ref, sum_ref):
    count = all_ref.shape[1]
    x, y = pos_ref[2], pos_ref[3]
    for d in range(4):
        for e, ref in ((0, mine_ref), (1, other_ref)):
            at = (((x + 4 - d) & 3) * 2 + (y ^ e)) * 2
            for comp in range(4):
                for j in range(2):
                    all_ref[comp, at + j] = ref[d, comp, j]
    base = (x * 2 + y) * 2
    factor = 1.0 / math.sqrt(count)
    for i in range(2):
        real, imag = 0.0, 0.0
        for v in range(count):
            ahead = (v + base + i) & (count - 1)
            behind = (v + count - base - i) & (count - 1)
            other_real = all_ref[2, ahead] + all_ref[2, behind]
            other_imag = all_ref[3, ahead] + all_ref[3, behind]
            real = real + all_ref[0, v] * other_real - all_ref[1, v] * other_imag
            imag = imag + all_ref[0, v] * other_imag + all_ref[1, v] * other_real
        sum_ref[4 * i : 4 * i + 4, :] = real * factor
        sum_ref[8 + 4 * i : 12 + 4 * i, :] = imag * factor
    sites = sum_ref.shape[1]
    rows = lax.broadcasted_iota(jnp.int32, (sites, site_ref.shape[1]), 0)
    hot = (rows == site_ref[...]).astype(jnp.float32).astype(jnp.bfloat16)
    whole = sum_ref[...]
    high = whole.astype(jnp.bfloat16)
    left = whole - high.astype(jnp.float32)
    middle = left.astype(jnp.bfloat16)
    low = (left - middle.astype(jnp.float32)).astype(jnp.bfloat16)
    out = jnp.dot(low, hot, preferred_element_type=jnp.float32)
    out = out + jnp.dot(middle, hot, preferred_element_type=jnp.float32)
    out_ref[...] = out + jnp.dot(high, hot, preferred_element_type=jnp.float32)


def bubble_of(pos, mine, other, sites):
    loop = 2 * 2 * mine.shape[0] * mine.shape[2] // 2
    return pl.pallas_call(
        bubble_kernel,
        in_specs=[SMEM, VMEM, VMEM, VMEM],
        out_specs=VMEM,
        out_shape=jax.ShapeDtypeStruct((16, sites.shape[1]), jnp.float32),
        scratch_shapes=[
            pltpu.VMEM((4, loop) + mine.shape[3:], jnp.float32),
            pltpu.VMEM((16, mine.shape[-1]), jnp.float32),
        ],
        compiler_params=params(),
        name="bubble",
    )(pos, mine, other, sites)


def flow_kernel(dzs, pos_ref, mask_ref, *refs):
    gammas, rights = (refs[0], refs[2]), (refs[1], refs[3])
    bubble_ref, perm_ref = refs[4:6]
    refs = refs[6:]
    outs, scratch = refs[:-1], refs[-1]
    planes = len(dzs)
    me = pos_ref[0]
    segs, order = gammas[0].shape[1:3]
    height = order // 8
    each = height // PLANE
    starts = [pl.multiple_of(((pos_ref[1] + dz) & 7) * height, 16) for dz in dzs]
    column = perm_ref[...] >> 7

    for w, gamma_ref, right_ref in zip(range(2), gammas, rights):
        keep = []
        for rb in range(3):
            m = [mask_ref[w, rb, cb] for cb in range(3)]
            keep.append(jnp.where(column == 0, m[0], jnp.where(column == 1, m[1], m[2])))
        masks = []
        for start in starts:
            block = (start + lax.broadcasted_iota(jnp.int32, (height, order), 0)) >> 7
            masks.append(jnp.where(block == 0, keep[0], jnp.where(block == 1, keep[1], keep[2])))
        mask = jnp.concatenate(masks, axis=0) != 0

        def one(s, carry, w=w, gamma_ref=gamma_ref, right_ref=right_ref, mask=mask):
            i = w * segs + s
            g_real, g_imag = [
                jnp.concatenate([gamma_ref[part, s, pl.ds(at, height), :] for at in starts], axis=0).astype(jnp.float32)
                for part in range(2)
            ]
            b_real = bubble_ref[pl.ds(i, 1), :]
            b_imag = bubble_ref[pl.ds(8 + i, 1), :]
            l_real = (g_real * b_real - g_imag * b_imag).astype(jnp.bfloat16)
            l_imag = (g_real * b_imag + g_imag * b_real).astype(jnp.bfloat16)
            dot = functools.partial(jnp.dot, preferred_element_type=jnp.float32)
            real = dot(l_real, right_ref[0, s]) - dot(l_imag, right_ref[1, s])
            imag = dot(l_real, right_ref[1, s]) + dot(l_imag, right_ref[0, s])
            for part, value in ((0, real), (1, imag)):
                value = jnp.where(mask, value, 0.0)
                for j in range(planes):
                    for p in range(PLANE):
                        at = j * height + p * each
                        scratch[part, j, p, s] = value[at : at + each]
            return carry

        if planes <= len(FIRST):
            for s in range(segs):
                one(s, 0)
        else:
            lax.fori_loop(0, segs, one, 0)
        for j in range(planes):
            for d in range(PLANE):
                for part in range(2):
                    rows = jnp.concatenate([scratch[part, j, d ^ me, s] for s in range(segs)], axis=0)
                    outs[j * PLANE + d][part, w] = rows.astype(jnp.bfloat16)


def flows(pos, mask, halves, bubble, perm, dzs):
    order = halves[0].shape[-1]
    planes = len(dzs)
    height = order // 8
    return pl.pallas_call(
        functools.partial(flow_kernel, dzs),
        in_specs=[SMEM, SMEM] + [VMEM] * (2 + len(halves)),
        out_specs=[VMEM] * (planes * PLANE),
        scratch_shapes=[pltpu.VMEM((2, planes, PLANE, halves[0].shape[1], height // PLANE, order), jnp.float32)],
        out_shape=[jax.ShapeDtypeStruct((2, 2, height, order), jnp.bfloat16)] * (planes * PLANE),
        compiler_params=params(),
        name="flow",
    )(pos, mask, *halves, bubble, perm)


def place_kernel(planes, pos_ref, *refs):
    out_ref, wide = refs[-2], refs[-1]
    height, order = refs[0].shape[2:]
    each = out_ref.shape[2]
    me = pos_ref[0]
    step, w = pl.program_id(0), pl.program_id(1)
    for j in range(planes):

        @pl.when(step == j)
        def _():
            for d in range(PLANE):
                at = pl.multiple_of((d ^ me) * height, 8)
                for part in range(2):
                    value = refs[j * PLANE + d][part, w].astype(jnp.float32)
                    for t in range(order // LANES):
                        wide[part, t, pl.ds(at, height), :] = value[:, t * LANES : (t + 1) * LANES]

    for part in range(2):
        for t in range(order // LANES):
            for r in range(each):
                rows = wide[part, t, pl.ds(r, 16, stride=each), :]
                out_ref[part, 0, r, :, t * LANES : (t + 1) * LANES] = rows.astype(jnp.bfloat16)


def place(pos, messages, so_far, shape, dzs):
    height, order = messages[0].shape[2:]
    each = height // PLANE
    planes = len(dzs)
    extra, aliases = [], {}
    if so_far is not None:
        extra, aliases = [so_far], {1 + PLANE * planes: 0}

    def target(j, w, p):
        dz = dzs[0]
        for k in range(1, planes):
            dz = dz + (dzs[k] - dzs[k - 1]) * (j >= k)
        return (0, w, 0, (p[1] + 8 - dz) & 7, 0)

    return pl.pallas_call(
        functools.partial(place_kernel, planes),
        grid_spec=pltpu.PrefetchScalarGridSpec(
            num_scalar_prefetch=1,
            grid=(planes, 2),
            in_specs=[VMEM] * (PLANE * planes) + [pl.BlockSpec(memory_space=pl.ANY)] * len(extra),
            out_specs=pl.BlockSpec((2, 1, each, 16, order), target),
            scratch_shapes=[pltpu.VMEM((2, order // LANES, PLANE * height, LANES), jnp.float32)],
        ),
        out_shape=jax.ShapeDtypeStruct(shape, jnp.bfloat16),
        input_output_aliases=aliases,
        compiler_params=params(),
        name="place",
    )(pos, *messages, *extra)


def steps(gamma, green, single, bond_site, causal_mask, site_perm):
    _, wide, segs, order, _ = gamma.shape
    bonds = lax.axis_size("bond")
    deep = bonds // PLANE
    bond, freq = lax.axis_index("bond"), lax.axis_index("freq")
    lane = lax.broadcasted_iota(jnp.int32, (4,), 0)
    pos = jnp.where(
        lane == 0,
        bond & 3,
        jnp.where(lane == 1, bond >> 2, jnp.where(lane == 2, freq >> 1, freq & 1)),
    )

    def along_x(a, d):
        return lax.ppermute(a, "freq", [(2 * x + y, 2 * ((x + d) % 4) + y) for x in range(4) for y in range(2)])

    zero = jnp.float32(0)
    none = ((0, 0, 0),) * 3
    own = lax.pad(green, zero, ((0, 2, 0),) + none) + lax.pad(single, zero, ((2, 0, 0),) + none)
    got = [own] + [along_x(own, d) for d in (1, 2, 3)]
    mine = jnp.stack(got)
    other = lax.ppermute(mine, "freq", [(i, i ^ 1) for i in range(8)])

    gamma = gamma.reshape(2, wide * segs, order, order)
    perm = site_perm.reshape(1, order)
    halves = spread(gamma, perm, 0)
    halves += spread(gamma, perm, 1)
    bubble = bubble_of(pos, mine, other, bond_site.reshape(1, order))

    received = {}
    for dzs in (FIRST, REST):
        sent = flows(pos, causal_mask, halves, bubble, perm, dzs)
        for j, dz in enumerate(dzs):
            for d in range(PLANE):
                m = sent[j * PLANE + d]
                if dz or d:
                    hops = [
                        (a * PLANE + p, ((a + dz) % deep) * PLANE + (p ^ d))
                        for a in range(deep)
                        for p in range(PLANE)
                    ]
                    m = lax.ppermute(m, "bond", hops)
                received[dz, d] = m
    out = None
    shape = (2, wide, order // bonds, bonds * segs, order)
    for dzs in GROUPS:
        out = place(pos, [received[dz, d] for dz in dzs for d in range(PLANE)], out, shape, dzs)
    return out


def solution(mesh):
    in_specs = (
        P(None, "freq", "bond", None, None),
        P(None, "freq", "bond", None),
        P(None, "freq", "bond", None),
        P(),
        P("freq", None, None),
        P(),
    )
    out_specs = P(None, "freq", "bond", None, None)
    return jax.shard_map(steps, mesh=mesh, in_specs=in_specs, out_specs=out_specs, check_vma=False)
```

time: 258 us -> 190 us (0.74)
  blocking collectives: 148 us -> 0 us
  starting transfers between devices: 0 us -> 127 us
  local copies, waits for them, and re-layouts: 71 us -> 9.96 us
  Pallas kernels: 0 us -> 27.5 us
  waiting for transfers between devices: 0 us -> 23.5 us
  matrix products: 23 us -> 0 us
  other arithmetic: 15 us -> 0.78 us
    ppermute x0 -> x35, starting transfers between devices: none -> 127 us  [the longest x31 121 us: steps(): m = lax.ppermute(m, 'bond', hops)]
    all_to_all x1 -> x0, blocking collectives: 125 us -> none  [body(): lax.all_to_all(flows, 'bond', split_axis=2, concat_axis=3, tiled=True)]
    gather x7 -> x0, local copies, waits for them, and re-layouts: 28.7 us -> none  [the longest x1 20.7 us: compute_flows(): return jnp.take(rounded, site_perm, axis=4)]
    pallas_call x0 -> x10, Pallas kernels: none -> 27.5 us  [the longest x5 10.1 us: place(): pl.pallas_call(functools.partial(place_kernel, planes), grid_spec=pltpu.P...]
    ppermute x0 -> x35, waiting for transfers between devices: none -> 23.5 us  [the longest x31 20 us: steps(): m = lax.ppermute(m, 'bond', hops)]
    all_gather x1 -> x0, blocking collectives: 23.4 us -> none  [side_by_side(): lax.all_gather(both, axis, axis=dim, tiled=True)]
    dot_general x4 -> x0, matrix products: 23 us -> none  [products(): return jnp.einsum(pattern, left, right, preferred_element_type=jnp.float32)]
    all_to_all x2 -> x0, local copies, waits for them, and re-layouts: 15 us -> none  [body(): lax.all_to_all(flows, 'bond', split_axis=2, concat_axis=3, tiled=True)]
  transfers between devices with their start and end apart: 0 -> 35, of which waited for: 0 -> 6; matrix products, arithmetic and copies ran while one was open for 0% -> 0% of each run, Pallas kernels for 0% -> 10%
where the time goes in v1:
time: 190 us; the launch traced here: 189 us
  starting transfers between devices  127 us (67%)
  Pallas kernels  27.5 us (14%)
  waiting for transfers between devices  23.5 us (12%)
  local copies, waits for them, and re-layouts  9.96 us (5%)
    ppermute x31, starting transfers between devices, steps(): m = lax.ppermute(m, 'bond', hops)  121 us
    ppermute x31, waiting for transfers between devices, steps(): m = lax.ppermute(m, 'bond', hops)  20 us
    pallas_call x5, Pallas kernels, place(): pl.pallas_call(functools.partial(place_kernel, planes), grid_spec=pltpu.P...  10.1 us
    pallas_call x2, Pallas kernels, flows(): pl.pallas_call(functools.partial(flow_kernel, dzs), in_specs=[SMEM, SMEM]...  9.88 us
    unnamed x17, local copies, waits for them, and re-layouts  9.27 us
    pallas_call x2, Pallas kernels, spread(): pl.pallas_call(functools.partial(spread_kernel, half * (count // 2)), in_...  6.75 us
    ppermute x3, starting transfers between devices, along_x(): lax.ppermute(a, 'freq', [(2 * x + y, 2 * ((x + d) % 4) + y) for x in rang...  4.5 us
  transfers between devices with their start and end apart: 35, of which 6 were waited for; matrix products, arithmetic and copies ran while one was open for 0% of the time, Pallas kernels for 10%

profile of v1, /device:TPU:1, one launch (start us, length us, event | category | flops | bytes accessed | tf_op | source)
XLA Modules:
  0.0 189.1 jit_solution(17396588751933371106)
XLA Ops:
  0.7 3.4 %collective-permute-start.2 = (f32[4,2,4,256]{3,2,1,0:T(4,128)S(1)}, f32[4,2,4,256]{3,2,1,0:T(4,128)S(1)}, u32[]{:S(2)}, u32[]{:S(2)}) collective-permute-start(f32[4,2,4,256]{3,2,1,0:T(4,128)S(1)} %get-tuple-element.78), channel_id=1, source_target_pairs={{0,192},{32,224},{64,0},{96,32},{128,64},{160,96},{192,128},{224,1... | collective-permute-start | bytes 98312 | tf_op jit(solution)/shard_map/ppermute | solution.py:246
  5.3 3.1 %collective-permute-done.1 = f32[4,2,4,256]{3,2,1,0:T(4,128)S(1)} collective-permute-done((f32[4,2,4,256]{3,2,1,0:T(4,128)S(1)}, f32[4,2,4,256]{3,2,1,0:T(4,128)S(1)}, u32[]{:S(2)}, u32[]{:S(2)}) %collective-permute-start.1) | collective-permute-done | bytes 32800 | tf_op jit(solution)/shard_map/ppermute | solution.py:246
  10.8 3.4 %spread.2 = (bf16[2,4,384,384]{3,2,1,0:T(8,128)(2,1)S(1)}, bf16[2,4,384,384]{3,2,1,0:T(8,128)(2,1)S(1)}) custom-call(s32[1,384]{1,0:T(1,128)S(1)} %reshape.9.perm_ref.refs_5_, bf16[2,8,384,384]{3,2,1,0:T(8,128)(2,1)} %bitcast.6), custom_call_target="tpu_custom_call" | custom-call | tf_op jit(solution)/shard_map/spread/pallas_call | solution.py:45
  15.7 3.4 %spread.3 = (bf16[2,4,384,384]{3,2,1,0:T(8,128)(2,1)S(1)}, bf16[2,4,384,384]{3,2,1,0:T(8,128)(2,1)S(1)}) custom-call(s32[1,384]{1,0:T(1,128)S(1)} %reshape.9.perm_ref.refs_5_, bf16[2,8,384,384]{3,2,1,0:T(8,128)(2,1)} %bitcast.7), custom_call_target="tpu_custom_call" | custom-call | tf_op jit(solution)/shard_map/spread/pallas_call | solution.py:45
  27.8 7.0 %flow.2 = (bf16[2,2,48,384]{3,2,1,0:T(8,128)(2,1)S(1)}, bf16[2,2,48,384]{3,2,1,0:T(8,128)(2,1)S(1)}, bf16[2,2,48,384]{3,2,1,0:T(8,128)(2,1)S(1)}, bf16[2,2,48,38...) custom-call(s32[4]{0:T(128)S(1)} %compare_select_fusion.2.pos_ref, ...), custom_call_target="tpu_custom_call" | custom-call | tf_op jit(solution)/shard_map/flow/pallas_call | solution.py:168
  44.3 3.9 %collective-permute-start.13 = (bf16[2,2,48,384]{3,2,1,0:T(8,128)(2,1)S(1)}, bf16[2,2,48,384]{3,2,1,0:T(8,128)(2,1)S(1)}, u32[]{:S(2)}, u32[]{:S(2)}) collective-permute-start(bf16[2,2,48,384]{3,2,1,0:T(8,128)(2,1)S(1)} %get-tuple-element.55), channel_id=1, source_target_pairs={{0,6},{1,7},{2,4},{3,5},{4,10},{5,11},{6,8},{7,9},{8,14},{9,15},{1... | collective-permute-start | bytes 442376 | tf_op jit(solution)/shard_map/ppermute | solution.py:273
  48.2 3.3 %collective-permute-start.15 = (bf16[2,2,48,384]{3,2,1,0:T(8,128)(2,1)S(1)}, bf16[2,2,48,384]{3,2,1,0:T(8,128)(2,1)S(1)}, u32[]{:S(2)}, u32[]{:S(2)}) collective-permute-start(bf16[2,2,48,384]{3,2,1,0:T(8,128)(2,1)S(1)} %get-tuple-element.57), channel_id=1, source_target_pairs={{0,8},{1,9},{2,10},{3,11},{4,12},{5,13},{6,14},{7,15},{8,16},{9,17... | collective-permute-start | bytes 442376 | tf_op jit(solution)/shard_map/ppermute | solution.py:273
  53.3 3.9 %collective-permute-start.17 = (bf16[2,2,48,384]{3,2,1,0:T(8,128)(2,1)S(1)}, bf16[2,2,48,384]{3,2,1,0:T(8,128)(2,1)S(1)}, u32[]{:S(2)}, u32[]{:S(2)}) collective-permute-start(bf16[2,2,48,384]{3,2,1,0:T(8,128)(2,1)S(1)} %get-tuple-element.59), channel_id=1, source_target_pairs={{0,10},{1,11},{2,8},{3,9},{4,14},{5,15},{6,12},{7,13},{8,18},{9,19... | collective-permute-start | bytes 442376 | tf_op jit(solution)/shard_map/ppermute | solution.py:273
  61.4 15.6 %collective-permute-start.20 = (bf16[2,2,48,384]{3,2,1,0:T(8,128)(2,1)S(1)}, bf16[2,2,48,384]{3,2,1,0:T(8,128)(2,1)S(1)}, u32[]{:S(2)}, u32[]{:S(2)}) collective-permute-start(bf16[2,2,48,384]{3,2,1,0:T(8,128)(2,1)S(1)} %get-tuple-element.62), channel_id=1, source_target_pairs={{0,25},{1,24},{2,27},{3,26},{4,29},{5,28},{6,31},{7,30},{8,1},{9,0... | collective-permute-start | bytes 442376 | tf_op jit(solution)/shard_map/ppermute | solution.py:273
  79.5 7.4 %collective-permute-start.23 = (bf16[2,2,48,384]{3,2,1,0:T(8,128)(2,1)S(1)}, bf16[2,2,48,384]{3,2,1,0:T(8,128)(2,1)S(1)}, u32[]{:S(2)}, u32[]{:S(2)}) collective-permute-start(bf16[2,2,48,384]{3,2,1,0:T(8,128)(2,1)S(1)} %get-tuple-element.65), channel_id=1, source_target_pairs={{0,16},{1,17},{2,18},{3,19},{4,20},{5,21},{6,22},{7,23},{8,24},{9,... | collective-permute-start | bytes 442376 | tf_op jit(solution)/shard_map/ppermute | solution.py:273
  87.4 2.9 %flow.3 = (bf16[2,2,48,384]{3,2,1,0:T(8,128)(2,1)S(1)}, bf16[2,2,48,384]{3,2,1,0:T(8,128)(2,1)S(1)}, bf16[2,2,48,384]{3,2,1,0:T(8,128)(2,1)S(1)}, bf16[2,2,48,38...) custom-call(s32[4]{0:T(128)S(1)} %compare_select_fusion.2.pos_ref, ...), custom_call_target="tpu_custom_call" | custom-call | tf_op jit(solution)/shard_map/flow/pallas_call | solution.py:168
  90.3 4.2 %collective-permute-start.25 = (bf16[2,2,48,384]{3,2,1,0:T(8,128)(2,1)S(1)}, bf16[2,2,48,384]{3,2,1,0:T(8,128)(2,1)S(1)}, u32[]{:S(2)}, u32[]{:S(2)}) collective-permute-start(bf16[2,2,48,384]{3,2,1,0:T(8,128)(2,1)S(1)} %get-tuple-element.67), channel_id=1, source_target_pairs={{0,18},{1,19},{2,16},{3,17},{4,22},{5,23},{6,20},{7,21},{8,26},{9,... | collective-permute-start | bytes 442376 | tf_op jit(solution)/shard_map/ppermute | solution.py:273
  94.4 4.7 %collective-permute-start.26 = (bf16[2,2,48,384]{3,2,1,0:T(8,128)(2,1)S(1)}, bf16[2,2,48,384]{3,2,1,0:T(8,128)(2,1)S(1)}, u32[]{:S(2)}, u32[]{:S(2)}) collective-permute-start(bf16[2,2,48,384]{3,2,1,0:T(8,128)(2,1)S(1)} %get-tuple-element.68), channel_id=1, source_target_pairs={{0,19},{1,18},{2,17},{3,16},{4,23},{5,22},{6,21},{7,20},{8,27},{9,... | collective-permute-start | bytes 442376 | tf_op jit(solution)/shard_map/ppermute | solution.py:273
  99.1 4.0 %collective-permute-start.27 = (bf16[2,2,48,384]{3,2,1,0:T(8,128)(2,1)S(1)}, bf16[2,2,48,384]{3,2,1,0:T(8,128)(2,1)S(1)}, u32[]{:S(2)}, u32[]{:S(2)}) collective-permute-start(bf16[2,2,48,384]{3,2,1,0:T(8,128)(2,1)S(1)} %get-tuple-element.69), channel_id=1, source_target_pairs={{0,12},{1,13},{2,14},{3,15},{4,16},{5,17},{6,18},{7,19},{8,20},{9,... | collective-permute-start | bytes 442376 | tf_op jit(solution)/shard_map/ppermute | solution.py:273
  103.1 25.7 %collective-permute-start.28 = (bf16[2,2,48,384]{3,2,1,0:T(8,128)(2,1)S(1)}, bf16[2,2,48,384]{3,2,1,0:T(8,128)(2,1)S(1)}, u32[]{:S(2)}, u32[]{:S(2)}) collective-permute-start(bf16[2,2,48,384]{3,2,1,0:T(8,128)(2,1)S(1)} %get-tuple-element.70), channel_id=1, source_target_pairs={{0,13},{1,12},{2,15},{3,14},{4,17},{5,16},{6,19},{7,18},{8,21},{9,... | collective-permute-start | bytes 442376 | tf_op jit(solution)/shard_map/ppermute | solution.py:273
  131.3 4.7 %collective-permute-start.31 = (bf16[2,2,48,384]{3,2,1,0:T(8,128)(2,1)S(1)}, bf16[2,2,48,384]{3,2,1,0:T(8,128)(2,1)S(1)}, u32[]{:S(2)}, u32[]{:S(2)}) collective-permute-start(bf16[2,2,48,384]{3,2,1,0:T(8,128)(2,1)S(1)} %get-tuple-element.73), channel_id=1, source_target_pairs={{0,20},{1,21},{2,22},{3,23},{4,24},{5,25},{6,26},{7,27},{8,28},{9,... | collective-permute-start | bytes 442376 | tf_op jit(solution)/shard_map/ppermute | solution.py:273
  136.0 4.7 %collective-permute-start.32 = (bf16[2,2,48,384]{3,2,1,0:T(8,128)(2,1)S(1)}, bf16[2,2,48,384]{3,2,1,0:T(8,128)(2,1)S(1)}, u32[]{:S(2)}, u32[]{:S(2)}) collective-permute-start(bf16[2,2,48,384]{3,2,1,0:T(8,128)(2,1)S(1)} %get-tuple-element.74), channel_id=1, source_target_pairs={{0,21},{1,20},{2,23},{3,22},{4,25},{5,24},{6,27},{7,26},{8,29},{9,... | collective-permute-start | bytes 442376 | tf_op jit(solution)/shard_map/ppermute | solution.py:273
  140.7 4.4 %collective-permute-start.33 = (bf16[2,2,48,384]{3,2,1,0:T(8,128)(2,1)S(1)}, bf16[2,2,48,384]{3,2,1,0:T(8,128)(2,1)S(1)}, u32[]{:S(2)}, u32[]{:S(2)}) collective-permute-start(bf16[2,2,48,384]{3,2,1,0:T(8,128)(2,1)S(1)} %get-tuple-element.75), channel_id=1, source_target_pairs={{0,22},{1,23},{2,20},{3,21},{4,26},{5,27},{6,24},{7,25},{8,30},{9,... | collective-permute-start | bytes 442376 | tf_op jit(solution)/shard_map/ppermute | solution.py:273
  145.1 6.3 %collective-permute-done.29.refs_2_ = bf16[2,2,48,384]{3,2,1,0:T(8,128)(2,1)S(1)} collective-permute-done((bf16[2,2,48,384]{3,2,1,0:T(8,128)(2,1)S(1)}, bf16[2,2,48,384]{3,2,1,0:T(8,128)(2,1)S(1)}, u32[]{:S(2)}, u32[]{:S(2)}) %collective-permute-start.29) | collective-permute-done | bytes 147488 | tf_op jit(solution)/shard_map/ppermute | solution.py:273
  152.2 6.2 %collective-permute-done.30.refs_3_ = bf16[2,2,48,384]{3,2,1,0:T(8,128)(2,1)S(1)} collective-permute-done((bf16[2,2,48,384]{3,2,1,0:T(8,128)(2,1)S(1)}, bf16[2,2,48,384]{3,2,1,0:T(8,128)(2,1)S(1)}, u32[]{:S(2)}, u32[]{:S(2)}) %collective-permute-start.30) | collective-permute-done | bytes 147488 | tf_op jit(solution)/shard_map/ppermute | solution.py:273
  158.4 9.1 %collective-permute-start.14 = (bf16[2,2,48,384]{3,2,1,0:T(8,128)(2,1)S(1)}, bf16[2,2,48,384]{3,2,1,0:T(8,128)(2,1)S(1)}, u32[]{:S(2)}, u32[]{:S(2)}) collective-permute-start(bf16[2,2,48,384]{3,2,1,0:T(8,128)(2,1)S(1)} %get-tuple-element.56), channel_id=1, source_target_pairs={{0,7},{1,6},{2,5},{3,4},{4,11},{5,10},{6,9},{7,8},{8,15},{9,14},{1... | collective-permute-start | bytes 442376 | tf_op jit(solution)/shard_map/ppermute | solution.py:273
  168.3 4.6 %collective-permute-done.34.refs_7_ = bf16[2,2,48,384]{3,2,1,0:T(8,128)(2,1)S(1)} collective-permute-done((bf16[2,2,48,384]{3,2,1,0:T(8,128)(2,1)S(1)}, bf16[2,2,48,384]{3,2,1,0:T(8,128)(2,1)S(1)}, u32[]{:S(2)}, u32[]{:S(2)}) %collective-permute-start.34) | collective-permute-done | bytes 147488 | tf_op jit(solution)/shard_map/ppermute | solution.py:273
  172.9 3.3 %collective-permute-start.7 = (bf16[2,2,48,384]{3,2,1,0:T(8,128)(2,1)S(1)}, bf16[2,2,48,384]{3,2,1,0:T(8,128)(2,1)S(1)}, u32[]{:S(2)}, u32[]{:S(2)}) collective-permute-start(bf16[2,2,48,384]{3,2,1,0:T(8,128)(2,1)S(1)} %get-tuple-element.48), channel_id=1, source_target_pairs={{0,31},{1,30},{2,29},{3,28},{4,3},{5,2},{6,1},{7,0},{8,7},{9,6},{1... | collective-permute-start | bytes 442376 | tf_op jit(solution)/shard_map/ppermute | solution.py:273
  184.8 2.8 %collective-permute-done.7.refs_3_ = bf16[2,2,48,384]{3,2,1,0:T(8,128)(2,1)S(1)} collective-permute-done((bf16[2,2,48,384]{3,2,1,0:T(8,128)(2,1)S(1)}, bf16[2,2,48,384]{3,2,1,0:T(8,128)(2,1)S(1)}, u32[]{:S(2)}, u32[]{:S(2)}) %collective-permute-start.7) | collective-permute-done | bytes 147488 | tf_op jit(solution)/shard_map/ppermute | solution.py:273
  (78 shorter events, 47.0 us)
Async XLA Ops:
  42.3 14.9 %collective-permute-start.12 = (bf16[2,2,48,384]{3,2,1,0:T(8,128)(2,1)S(1)}, bf16[2,2,48,384]{3,2,1,0:T(8,128)(2,1)S(1)}, u32[]{:S(2)}, u32[]{:S(2)}) collective-permute-start(bf16[2,2,48,384]{3,2,1,0:T(8,128)(2,1)S(1)} %get-tuple-element.54), channel_id=1, source_target_pairs={{0,5},{1,4},{2,7},{3,6},{4,9},{5,8},{6,11},{7,10},{8,13},{9,12},{1... | collective-permute-start | bytes 442376 | tf_op jit(solution)/shard_map/ppermute | solution.py:273
  51.5 25.5 %collective-permute-start.16 = (bf16[2,2,48,384]{3,2,1,0:T(8,128)(2,1)S(1)}, bf16[2,2,48,384]{3,2,1,0:T(8,128)(2,1)S(1)}, u32[]{:S(2)}, u32[]{:S(2)}) collective-permute-start(bf16[2,2,48,384]{3,2,1,0:T(8,128)(2,1)S(1)} %get-tuple-element.58), channel_id=1, source_target_pairs={{0,9},{1,8},{2,11},{3,10},{4,13},{5,12},{6,15},{7,14},{8,17},{9,16... | collective-permute-start | bytes 442376 | tf_op jit(solution)/shard_map/ppermute | solution.py:273
  53.3 23.9 %collective-permute-start.17 = (bf16[2,2,48,384]{3,2,1,0:T(8,128)(2,1)S(1)}, bf16[2,2,48,384]{3,2,1,0:T(8,128)(2,1)S(1)}, u32[]{:S(2)}, u32[]{:S(2)}) collective-permute-start(bf16[2,2,48,384]{3,2,1,0:T(8,128)(2,1)S(1)} %get-tuple-element.59), channel_id=1, source_target_pairs={{0,10},{1,11},{2,8},{3,9},{4,14},{5,15},{6,12},{7,13},{8,18},{9,19... | collective-permute-start | bytes 442376 | tf_op jit(solution)/shard_map/ppermute | solution.py:273
  57.2 22.3 %collective-permute-start.18 = (bf16[2,2,48,384]{3,2,1,0:T(8,128)(2,1)S(1)}, bf16[2,2,48,384]{3,2,1,0:T(8,128)(2,1)S(1)}, u32[]{:S(2)}, u32[]{:S(2)}) collective-permute-start(bf16[2,2,48,384]{3,2,1,0:T(8,128)(2,1)S(1)} %get-tuple-element.60), channel_id=1, source_target_pairs={{0,11},{1,10},{2,9},{3,8},{4,15},{5,14},{6,13},{7,12},{8,19},{9,18... | collective-permute-start | bytes 442376 | tf_op jit(solution)/shard_map/ppermute | solution.py:273
  59.1 27.9 %collective-permute-start.19 = (bf16[2,2,48,384]{3,2,1,0:T(8,128)(2,1)S(1)}, bf16[2,2,48,384]{3,2,1,0:T(8,128)(2,1)S(1)}, u32[]{:S(2)}, u32[]{:S(2)}) collective-permute-start(bf16[2,2,48,384]{3,2,1,0:T(8,128)(2,1)S(1)} %get-tuple-element.61), channel_id=1, source_target_pairs={{0,24},{1,25},{2,26},{3,27},{4,28},{5,29},{6,30},{7,31},{8,0},{9,1... | collective-permute-start | bytes 442376 | tf_op jit(solution)/shard_map/ppermute | solution.py:273
  61.4 28.8 %collective-permute-start.20 = (bf16[2,2,48,384]{3,2,1,0:T(8,128)(2,1)S(1)}, bf16[2,2,48,384]{3,2,1,0:T(8,128)(2,1)S(1)}, u32[]{:S(2)}, u32[]{:S(2)}) collective-permute-start(bf16[2,2,48,384]{3,2,1,0:T(8,128)(2,1)S(1)} %get-tuple-element.62), channel_id=1, source_target_pairs={{0,25},{1,24},{2,27},{3,26},{4,29},{5,28},{6,31},{7,30},{8,1},{9,0... | collective-permute-start | bytes 442376 | tf_op jit(solution)/shard_map/ppermute | solution.py:273
  77.0 17.4 %collective-permute-start.21 = (bf16[2,2,48,384]{3,2,1,0:T(8,128)(2,1)S(1)}, bf16[2,2,48,384]{3,2,1,0:T(8,128)(2,1)S(1)}, u32[]{:S(2)}, u32[]{:S(2)}) collective-permute-start(bf16[2,2,48,384]{3,2,1,0:T(8,128)(2,1)S(1)} %get-tuple-element.63), channel_id=1, source_target_pairs={{0,26},{1,27},{2,24},{3,25},{4,30},{5,31},{6,28},{7,29},{8,2},{9,3... | collective-permute-start | bytes 442376 | tf_op jit(solution)/shard_map/ppermute | solution.py:273
  77.2 21.9 %collective-permute-start.22 = (bf16[2,2,48,384]{3,2,1,0:T(8,128)(2,1)S(1)}, bf16[2,2,48,384]{3,2,1,0:T(8,128)(2,1)S(1)}, u32[]{:S(2)}, u32[]{:S(2)}) collective-permute-start(bf16[2,2,48,384]{3,2,1,0:T(8,128)(2,1)S(1)} %get-tuple-element.64), channel_id=1, source_target_pairs={{0,27},{1,26},{2,25},{3,24},{4,31},{5,30},{6,29},{7,28},{8,3},{9,2... | collective-permute-start | bytes 442376 | tf_op jit(solution)/shard_map/ppermute | solution.py:273
  79.5 23.6 %collective-permute-start.23 = (bf16[2,2,48,384]{3,2,1,0:T(8,128)(2,1)S(1)}, bf16[2,2,48,384]{3,2,1,0:T(8,128)(2,1)S(1)}, u32[]{:S(2)}, u32[]{:S(2)}) collective-permute-start(bf16[2,2,48,384]{3,2,1,0:T(8,128)(2,1)S(1)} %get-tuple-element.65), channel_id=1, source_target_pairs={{0,16},{1,17},{2,18},{3,19},{4,20},{5,21},{6,22},{7,23},{8,24},{9,... | collective-permute-start | bytes 442376 | tf_op jit(solution)/shard_map/ppermute | solution.py:273
  86.9 41.8 %collective-permute-start.24 = (bf16[2,2,48,384]{3,2,1,0:T(8,128)(2,1)S(1)}, bf16[2,2,48,384]{3,2,1,0:T(8,128)(2,1)S(1)}, u32[]{:S(2)}, u32[]{:S(2)}) collective-permute-start(bf16[2,2,48,384]{3,2,1,0:T(8,128)(2,1)S(1)} %get-tuple-element.66), channel_id=1, source_target_pairs={{0,17},{1,16},{2,19},{3,18},{4,21},{5,20},{6,23},{7,22},{8,25},{9,... | collective-permute-start | bytes 442376 | tf_op jit(solution)/shard_map/ppermute | solution.py:273
  90.3 38.5 %collective-permute-start.25 = (bf16[2,2,48,384]{3,2,1,0:T(8,128)(2,1)S(1)}, bf16[2,2,48,384]{3,2,1,0:T(8,128)(2,1)S(1)}, u32[]{:S(2)}, u32[]{:S(2)}) collective-permute-start(bf16[2,2,48,384]{3,2,1,0:T(8,128)(2,1)S(1)} %get-tuple-element.67), channel_id=1, source_target_pairs={{0,18},{1,19},{2,16},{3,17},{4,22},{5,23},{6,20},{7,21},{8,26},{9,... | collective-permute-start | bytes 442376 | tf_op jit(solution)/shard_map/ppermute | solution.py:273
  94.4 36.8 %collective-permute-start.26 = (bf16[2,2,48,384]{3,2,1,0:T(8,128)(2,1)S(1)}, bf16[2,2,48,384]{3,2,1,0:T(8,128)(2,1)S(1)}, u32[]{:S(2)}, u32[]{:S(2)}) collective-permute-start(bf16[2,2,48,384]{3,2,1,0:T(8,128)(2,1)S(1)} %get-tuple-element.68), channel_id=1, source_target_pairs={{0,19},{1,18},{2,17},{3,16},{4,23},{5,22},{6,21},{7,20},{8,27},{9,... | collective-permute-start | bytes 442376 | tf_op jit(solution)/shard_map/ppermute | solution.py:273
  99.1 36.9 %collective-permute-start.27 = (bf16[2,2,48,384]{3,2,1,0:T(8,128)(2,1)S(1)}, bf16[2,2,48,384]{3,2,1,0:T(8,128)(2,1)S(1)}, u32[]{:S(2)}, u32[]{:S(2)}) collective-permute-start(bf16[2,2,48,384]{3,2,1,0:T(8,128)(2,1)S(1)} %get-tuple-element.69), channel_id=1, source_target_pairs={{0,12},{1,13},{2,14},{3,15},{4,16},{5,17},{6,18},{7,19},{8,20},{9,... | collective-permute-start | bytes 442376 | tf_op jit(solution)/shard_map/ppermute | solution.py:273
  103.1 37.6 %collective-permute-start.28 = (bf16[2,2,48,384]{3,2,1,0:T(8,128)(2,1)S(1)}, bf16[2,2,48,384]{3,2,1,0:T(8,128)(2,1)S(1)}, u32[]{:S(2)}, u32[]{:S(2)}) collective-permute-start(bf16[2,2,48,384]{3,2,1,0:T(8,128)(2,1)S(1)} %get-tuple-element.70), channel_id=1, source_target_pairs={{0,13},{1,12},{2,15},{3,14},{4,17},{5,16},{6,19},{7,18},{8,21},{9,... | collective-permute-start | bytes 442376 | tf_op jit(solution)/shard_map/ppermute | solution.py:273
  128.8 22.6 %collective-permute-start.29 = (bf16[2,2,48,384]{3,2,1,0:T(8,128)(2,1)S(1)}, bf16[2,2,48,384]{3,2,1,0:T(8,128)(2,1)S(1)}, u32[]{:S(2)}, u32[]{:S(2)}) collective-permute-start(bf16[2,2,48,384]{3,2,1,0:T(8,128)(2,1)S(1)} %get-tuple-element.71), channel_id=1, source_target_pairs={{0,14},{1,15},{2,12},{3,13},{4,18},{5,19},{6,16},{7,17},{8,22},{9,... | collective-permute-start | bytes 442376 | tf_op jit(solution)/shard_map/ppermute | solution.py:273
  128.8 29.6 %collective-permute-start.30 = (bf16[2,2,48,384]{3,2,1,0:T(8,128)(2,1)S(1)}, bf16[2,2,48,384]{3,2,1,0:T(8,128)(2,1)S(1)}, u32[]{:S(2)}, u32[]{:S(2)}) collective-permute-start(bf16[2,2,48,384]{3,2,1,0:T(8,128)(2,1)S(1)} %get-tuple-element.72), channel_id=1, source_target_pairs={{0,15},{1,14},{2,13},{3,12},{4,19},{5,18},{6,17},{7,16},{8,23},{9,... | collective-permute-start | bytes 442376 | tf_op jit(solution)/shard_map/ppermute | solution.py:273
  131.3 27.1 %collective-permute-start.31 = (bf16[2,2,48,384]{3,2,1,0:T(8,128)(2,1)S(1)}, bf16[2,2,48,384]{3,2,1,0:T(8,128)(2,1)S(1)}, u32[]{:S(2)}, u32[]{:S(2)}) collective-permute-start(bf16[2,2,48,384]{3,2,1,0:T(8,128)(2,1)S(1)} %get-tuple-element.73), channel_id=1, source_target_pairs={{0,20},{1,21},{2,22},{3,23},{4,24},{5,25},{6,26},{7,27},{8,28},{9,... | collective-permute-start | bytes 442376 | tf_op jit(solution)/shard_map/ppermute | solution.py:273
  136.0 22.4 %collective-permute-start.32 = (bf16[2,2,48,384]{3,2,1,0:T(8,128)(2,1)S(1)}, bf16[2,2,48,384]{3,2,1,0:T(8,128)(2,1)S(1)}, u32[]{:S(2)}, u32[]{:S(2)}) collective-permute-start(bf16[2,2,48,384]{3,2,1,0:T(8,128)(2,1)S(1)} %get-tuple-element.74), channel_id=1, source_target_pairs={{0,21},{1,20},{2,23},{3,22},{4,25},{5,24},{6,27},{7,26},{8,29},{9,... | collective-permute-start | bytes 442376 | tf_op jit(solution)/shard_map/ppermute | solution.py:273
  140.7 26.8 %collective-permute-start.33 = (bf16[2,2,48,384]{3,2,1,0:T(8,128)(2,1)S(1)}, bf16[2,2,48,384]{3,2,1,0:T(8,128)(2,1)S(1)}, u32[]{:S(2)}, u32[]{:S(2)}) collective-permute-start(bf16[2,2,48,384]{3,2,1,0:T(8,128)(2,1)S(1)} %get-tuple-element.75), channel_id=1, source_target_pairs={{0,22},{1,23},{2,20},{3,21},{4,26},{5,27},{6,24},{7,25},{8,30},{9,... | collective-permute-start | bytes 442376 | tf_op jit(solution)/shard_map/ppermute | solution.py:273
  151.4 21.5 %collective-permute-start.34 = (bf16[2,2,48,384]{3,2,1,0:T(8,128)(2,1)S(1)}, bf16[2,2,48,384]{3,2,1,0:T(8,128)(2,1)S(1)}, u32[]{:S(2)}, u32[]{:S(2)}) collective-permute-start(bf16[2,2,48,384]{3,2,1,0:T(8,128)(2,1)S(1)} %get-tuple-element.76), channel_id=1, source_target_pairs={{0,23},{1,22},{2,21},{3,20},{4,27},{5,26},{6,25},{7,24},{8,31},{9,... | collective-permute-start | bytes 442376 | tf_op jit(solution)/shard_map/ppermute | solution.py:273
  158.4 26.4 %collective-permute-start.4 = (bf16[2,2,48,384]{3,2,1,0:T(8,128)(2,1)S(1)}, bf16[2,2,48,384]{3,2,1,0:T(8,128)(2,1)S(1)}, u32[]{:S(2)}, u32[]{:S(2)}) collective-permute-start(bf16[2,2,48,384]{3,2,1,0:T(8,128)(2,1)S(1)} %get-tuple-element.45), channel_id=1, source_target_pairs={{0,28},{1,29},{2,30},{3,31},{4,0},{5,1},{6,2},{7,3},{8,4},{9,5},{1... | collective-permute-start | bytes 442376 | tf_op jit(solution)/shard_map/ppermute | solution.py:273
  158.4 26.4 %collective-permute-start.5 = (bf16[2,2,48,384]{3,2,1,0:T(8,128)(2,1)S(1)}, bf16[2,2,48,384]{3,2,1,0:T(8,128)(2,1)S(1)}, u32[]{:S(2)}, u32[]{:S(2)}) collective-permute-start(bf16[2,2,48,384]{3,2,1,0:T(8,128)(2,1)S(1)} %get-tuple-element.46), channel_id=1, source_target_pairs={{0,29},{1,28},{2,31},{3,30},{4,1},{5,0},{6,3},{7,2},{8,5},{9,4},{1... | collective-permute-start | bytes 442376 | tf_op jit(solution)/shard_map/ppermute | solution.py:273
  158.4 24.0 %collective-permute-start.14 = (bf16[2,2,48,384]{3,2,1,0:T(8,128)(2,1)S(1)}, bf16[2,2,48,384]{3,2,1,0:T(8,128)(2,1)S(1)}, u32[]{:S(2)}, u32[]{:S(2)}) collective-permute-start(bf16[2,2,48,384]{3,2,1,0:T(8,128)(2,1)S(1)} %get-tuple-element.56), channel_id=1, source_target_pairs={{0,7},{1,6},{2,5},{3,4},{4,11},{5,10},{6,9},{7,8},{8,15},{9,14},{1... | collective-permute-start | bytes 442376 | tf_op jit(solution)/shard_map/ppermute | solution.py:273
  167.6 17.3 %collective-permute-start.6 = (bf16[2,2,48,384]{3,2,1,0:T(8,128)(2,1)S(1)}, bf16[2,2,48,384]{3,2,1,0:T(8,128)(2,1)S(1)}, u32[]{:S(2)}, u32[]{:S(2)}) collective-permute-start(bf16[2,2,48,384]{3,2,1,0:T(8,128)(2,1)S(1)} %get-tuple-element.47), channel_id=1, source_target_pairs={{0,30},{1,31},{2,28},{3,29},{4,2},{5,3},{6,0},{7,1},{8,6},{9,7},{1... | collective-permute-start | bytes 442376 | tf_op jit(solution)/shard_map/ppermute | solution.py:273
  (19 other events, 144.5 us)

commit v2 on v1

v2 whole, which is shorter than its diff:
```python
import functools
import math

import jax
import jax.numpy as jnp
from jax import lax
from jax.experimental import pallas as pl
from jax.experimental.pallas import tpu as pltpu
from jax.sharding import PartitionSpec as P


PLANE = 4
HALF = (4,)
FAR = (3, 5)
LATE = (2, 6, 1, 7, 0)
VMEM = pl.BlockSpec(memory_space=pltpu.VMEM)
SMEM = pl.BlockSpec(memory_space=pltpu.SMEM)


def params(mib=24):
    return pltpu.CompilerParams(vmem_limit_bytes=mib * 1024 * 1024)


def tables_kernel(pos_ref, perm_ref, gamma_ref, near_ref, hot_ref, rows_ref, sem):
    copy = pltpu.make_async_copy(gamma_ref, near_ref, sem)
    copy.start()
    order = hot_ref.shape[0]
    source = lax.broadcasted_iota(jnp.int32, (order, order), 0)
    hot_ref[...] = (source == perm_ref[...]).astype(jnp.float32).astype(jnp.bfloat16)
    count = rows_ref.shape[0]
    each = count // 16

    def over(value, unit):
        return sum((value >= unit * k).astype(jnp.int32) for k in range(1, 4))

    at = lax.broadcasted_iota(jnp.int32, (1, count), 1)
    device = over(at, 4 * each)
    at = at - 4 * each * device
    seg = over(at, each)
    target = (at - each * seg) * 16 + (device ^ pos_ref[0]) * 4 + seg
    row = lax.broadcasted_iota(jnp.int32, (count, count), 0)
    rows_ref[...] = (row == target).astype(jnp.float32).astype(jnp.bfloat16)
    copy.wait()


def tables(pos, perm, gamma):
    order = perm.shape[1]
    return pl.pallas_call(
        tables_kernel,
        in_specs=[SMEM, VMEM, pl.BlockSpec(memory_space=pltpu.HBM)],
        out_specs=[VMEM, VMEM, VMEM],
        out_shape=[
            jax.ShapeDtypeStruct(gamma.shape, gamma.dtype),
            jax.ShapeDtypeStruct((order, order), jnp.bfloat16),
            jax.ShapeDtypeStruct((order // 2, order // 2), jnp.bfloat16),
        ],
        scratch_shapes=[pltpu.SemaphoreType.DMA],
        compiler_params=params(48),
        name="tables",
    )(pos, perm, gamma)


def bubble_kernel(pos_ref, mine_ref, other_ref, site_ref, out_ref, all_ref, sum_ref):
    count = all_ref.shape[1]
    x, y = pos_ref[2], pos_ref[3]
    for d in range(4):
        for e, ref in ((0, mine_ref), (1, other_ref)):
            at = (((x + 4 - d) & 3) * 2 + (y ^ e)) * 2
            for comp in range(4):
                for j in range(2):
                    all_ref[comp, at + j] = ref[d, comp, j]
    base = (x * 2 + y) * 2
    factor = 1.0 / math.sqrt(count)
    for i in range(2):
        real, imag = 0.0, 0.0
        for v in range(count):
            ahead = (v + base + i) & (count - 1)
            behind = (v + count - base - i) & (count - 1)
            other_real = all_ref[2, ahead] + all_ref[2, behind]
            other_imag = all_ref[3, ahead] + all_ref[3, behind]
            real = real + all_ref[0, v] * other_real - all_ref[1, v] * other_imag
            imag = imag + all_ref[0, v] * other_imag + all_ref[1, v] * other_real
        sum_ref[4 * i : 4 * i + 4, :] = real * factor
        sum_ref[8 + 4 * i : 12 + 4 * i, :] = imag * factor
    sites = sum_ref.shape[1]
    rows = lax.broadcasted_iota(jnp.int32, (sites, site_ref.shape[1]), 0)
    hot = (rows == site_ref[...]).astype(jnp.float32).astype(jnp.bfloat16)
    whole = sum_ref[...]
    high = whole.astype(jnp.bfloat16)
    left = whole - high.astype(jnp.float32)
    middle = left.astype(jnp.bfloat16)
    low = (left - middle.astype(jnp.float32)).astype(jnp.bfloat16)
    out = jnp.dot(low, hot, preferred_element_type=jnp.float32)
    out = out + jnp.dot(middle, hot, preferred_element_type=jnp.float32)
    out_ref[...] = out + jnp.dot(high, hot, preferred_element_type=jnp.float32)


def bubble_of(pos, mine, other, sites):
    loop = 2 * 2 * mine.shape[0] * mine.shape[2] // 2
    return pl.pallas_call(
        bubble_kernel,
        in_specs=[SMEM, VMEM, VMEM, VMEM],
        out_specs=VMEM,
        out_shape=jax.ShapeDtypeStruct((16, sites.shape[1]), jnp.float32),
        scratch_shapes=[
            pltpu.VMEM((4, loop) + mine.shape[3:], jnp.float32),
            pltpu.VMEM((16, mine.shape[-1]), jnp.float32),
        ],
        compiler_params=params(),
        name="bubble",
    )(pos, mine, other, sites)


def flow_kernel(dzs, by_plane, unroll, pos_ref, mask_ref, gamma_ref, bubble_ref, *refs):
    hot_ref, *outs, scratch = refs if unroll is False else (None, *refs)
    planes = len(dzs)
    me = pos_ref[0]
    order = gamma_ref.shape[-1]
    segs = gamma_ref.shape[1] // 2
    height = order // 8
    each = height // PLANE
    starts = [pl.multiple_of(((pos_ref[1] + dz) & 7) * height, 16) for dz in dzs]
    column = lax.broadcasted_iota(jnp.int32, (1, order), 1) >> 7

    for w in range(2):
        keep = []
        for rb in range(3):
            m = [mask_ref[w, rb, cb] for cb in range(3)]
            keep.append(jnp.where(column == 0, m[0], jnp.where(column == 1, m[1], m[2])))
        masks = []
        for start in starts:
            block = (start + lax.broadcasted_iota(jnp.int32, (height, order), 0)) >> 7
            masks.append(jnp.where(block == 0, keep[0], jnp.where(block == 1, keep[1], keep[2])))
        mask = jnp.concatenate(masks, axis=0) != 0

        def one(s, carry, w=w, mask=mask):
            i = w * segs + s
            g_real, g_imag = [
                jnp.concatenate([gamma_ref[part, i, pl.ds(at, height), :] for at in starts], axis=0).astype(jnp.float32)
                for part in range(2)
            ]
            b_real = bubble_ref[pl.ds(i, 1), :]
            b_imag = bubble_ref[pl.ds(8 + i, 1), :]
            l_real = (g_real * b_real - g_imag * b_imag).astype(jnp.bfloat16)
            l_imag = (g_real * b_imag + g_imag * b_real).astype(jnp.bfloat16)
            dot = functools.partial(jnp.dot, preferred_element_type=jnp.float32)
            real = dot(l_real, gamma_ref[0, i]) - dot(l_imag, gamma_ref[1, i])
            imag = dot(l_real, gamma_ref[1, i]) + dot(l_imag, gamma_ref[0, i])
            values = [jnp.where(mask, value, 0.0) for value in (real, imag)]
            if hot_ref is not None:
                both = dot(jnp.concatenate(values, axis=0).astype(jnp.bfloat16), hot_ref[...])
                values = [both[: planes * height], both[planes * height :]]
            for part, value in enumerate(values):
                for j in range(planes):
                    for p in range(PLANE):
                        at = j * height + p * each
                        scratch[part, j, p, s] = value[at : at + each]
            return carry

        if unroll:
            for s in range(segs):
                one(s, 0)
        else:
            lax.fori_loop(0, segs, one, 0)
        for j in range(planes):
            for d in range(PLANE):
                for part in range(2):
                    rows = jnp.concatenate([scratch[part, j, d ^ me, s] for s in range(segs)], axis=0)
                    out = outs[j].at[d] if by_plane else outs[d].at[j]
                    out[part, w] = rows.astype(jnp.bfloat16)


def flows(pos, mask, gamma, bubble, dzs, by_plane, *hot):
    _, count, order, _ = gamma.shape
    segs = count // 2
    planes = len(dzs)
    height = order // 8
    number, inner = (planes, PLANE) if by_plane else (PLANE, planes)
    return pl.pallas_call(
        functools.partial(flow_kernel, dzs, by_plane, not hot),
        in_specs=[SMEM, SMEM, VMEM, VMEM] + [VMEM] * len(hot),
        out_specs=[VMEM] * number,
        scratch_shapes=[pltpu.VMEM((2, planes, PLANE, segs, height // PLANE, order), jnp.float32)],
        out_shape=[jax.ShapeDtypeStruct((inner, 2, 2, height, order), jnp.bfloat16)] * number,
        compiler_params=params(),
        name="flow",
    )(pos, mask, gamma, bubble, *hot)


def turn(arrays, outer):
    _, *rest = arrays[0].shape
    shape = jax.ShapeDtypeStruct((len(arrays), *rest), arrays[0].dtype)

    def kernel(*refs):
        ins, outs = refs[: len(arrays)], refs[len(arrays) :]
        for out, b in zip(outs, outer):
            for a, ref in enumerate(ins):
                out[a] = ref[b]

    return pl.pallas_call(
        kernel,
        in_specs=[VMEM] * len(arrays),
        out_specs=[VMEM] * len(outer),
        out_shape=[shape] * len(outer),
        compiler_params=params(),
        name="turn",
    )(*arrays)


def place_kernel(units, columns, pos_ref, hot_ref, rows_ref, *refs):
    out_ref, wide = refs[-2:]
    height, _ = refs[0].shape[3:]
    count = PLANE * height
    step, w = pl.program_id(0), pl.program_id(1)
    for j in range(len(units)):

        @pl.when(step == j)
        def _():
            for d in range(PLANE):
                array, lead = units[j][d]
                for part in range(2):
                    wide[part, d * height : (d + 1) * height, :] = refs[array][lead, part, w]

    dot = functools.partial(jnp.dot, preferred_element_type=jnp.float32)
    rows = [dot(rows_ref[...], wide[part]).astype(jnp.bfloat16) for part in range(2)]
    if columns:
        both = dot(jnp.concatenate(rows, axis=0), hot_ref[...]).astype(jnp.bfloat16)
        rows = [both[:count], both[count:]]
    for part in range(2):
        out_ref[part, 0] = rows[part].reshape(out_ref.shape[2:])


def place(pos, ones, arrays, units, so_far, shape, dzs):
    height, order = arrays[0].shape[3:]
    each = height // PLANE
    extra, aliases = [], {}
    if so_far is not None:
        extra, aliases = [so_far], {3 + len(arrays): 0}

    def target(j, w, p):
        dz = dzs[0]
        for k in range(1, len(dzs)):
            dz = dz + (dzs[k] - dzs[k - 1]) * (j >= k)
        return (0, w, 0, (p[1] + 8 - dz) & 7, 0)

    return pl.pallas_call(
        functools.partial(place_kernel, units, dzs[0] not in LATE),
        grid_spec=pltpu.PrefetchScalarGridSpec(
            num_scalar_prefetch=1,
            grid=(len(dzs), 2),
            in_specs=[VMEM] * (2 + len(arrays)) + [pl.BlockSpec(memory_space=pl.ANY)] * len(extra),
            out_specs=pl.BlockSpec((2, 1, each, 16, order), target),
            scratch_shapes=[pltpu.VMEM((2, PLANE * height, order), jnp.bfloat16)],
        ),
        out_shape=jax.ShapeDtypeStruct(shape, jnp.bfloat16),
        input_output_aliases=aliases,
        compiler_params=params(),
        name="place",
    )(pos, *ones, *arrays, *extra)


def steps(gamma, green, single, bond_site, causal_mask, site_perm):
    _, wide, segs, order, _ = gamma.shape
    bonds = lax.axis_size("bond")
    deep = bonds // PLANE
    bond, freq = lax.axis_index("bond"), lax.axis_index("freq")
    lane = lax.broadcasted_iota(jnp.int32, (4,), 0)
    pos = jnp.where(
        lane == 0,
        bond & 3,
        jnp.where(lane == 1, bond >> 2, jnp.where(lane == 2, freq >> 1, freq & 1)),
    )

    def along_x(a, d):
        return lax.ppermute(a, "freq", [(2 * x + y, 2 * ((x + d) % 4) + y) for x in range(4) for y in range(2)])

    zero = jnp.float32(0)
    none = ((0, 0, 0),) * 3
    own = lax.pad(green, zero, ((0, 2, 0),) + none) + lax.pad(single, zero, ((2, 0, 0),) + none)
    got = [own] + [along_x(own, d) for d in (1, 2, 3)]
    mine = jnp.stack(got)
    other = lax.ppermute(mine, "freq", [(i, i ^ 1) for i in range(8)])

    gamma = gamma.reshape(2, wide * segs, order, order)
    perm = site_perm.reshape(1, order)
    sites = bond_site.reshape(1, order)
    gamma, *ones = tables(pos, perm, gamma)
    bubble = bubble_of(pos, mine, other, sites)

    def along_z(a, dz):
        hops = [(i * PLANE + p, ((i + dz) % deep) * PLANE + p) for i in range(deep) for p in range(PLANE)]
        return lax.ppermute(a, "bond", hops)

    def in_plane(a, d):
        return lax.ppermute(a, "bond", [(i, i ^ d) for i in range(bonds)])

    flow = functools.partial(flows, pos, causal_mask, gamma, bubble)
    early = []
    for dzs in (HALF, FAR):
        bundles = flow(dzs, True)
        early += [along_z(a, dz) for a, dz in zip(bundles, dzs)]
    sets = flow(LATE, False, ones[0])
    sets = [sets[0]] + [in_plane(sets[d], d) for d in range(1, PLANE)]
    bundles = turn(sets, range(len(LATE) - 1))
    late = [along_z(a, dz) for a, dz in zip(bundles, LATE)]
    back = turn(early, range(1, PLANE))
    back = [in_plane(a, d) for d, a in enumerate(back, 1)]

    shape = (2, wide, order // bonds, bonds * segs, order)
    last = len(LATE) - 1
    put = functools.partial(place, pos, ones)
    out = put(sets, [[(d, last) for d in range(PLANE)]], None, shape, LATE[last:])
    units = [[(j, 0)] + [(len(early) + d, j) for d in range(PLANE - 1)] for j in range(len(early))]
    out = put(early + back, units, out, shape, HALF + FAR)
    units = [[(j % 2, d) for d in range(PLANE)] for j in range(last)]
    out = put(late[:2], units[:2], out, shape, LATE[:2])
    return put(late[2:], units[2:], out, shape, LATE[2:last])


def solution(mesh):
    in_specs = (
        P(None, "freq", "bond", None, None),
        P(None, "freq", "bond", None),
        P(None, "freq", "bond", None),
        P(),
        P("freq", None, None),
        P(),
    )
    out_specs = P(None, "freq", "bond", None, None)
    return jax.shard_map(steps, mesh=mesh, in_specs=in_specs, out_specs=out_specs, check_vma=False)
```

time: 190 us -> 140 us (0.74)
  starting transfers between devices: 127 us -> 56.4 us
  waiting for transfers between devices: 23.5 us -> 49.5 us
  local copies, waits for them, and re-layouts: 9.96 us -> 2.05 us
  Pallas kernels: 27.5 us -> 30.2 us
    ppermute x31 -> x13, starting transfers between devices: 121 us -> 49 us  [the longest x6 32 us: in_plane(): return lax.ppermute(a, 'bond', [(i, i ^ d) for i in range(bonds)])]
    ppermute x31 -> x13, waiting for transfers between devices: 20 us -> 47.9 us  [the longest x7 33.9 us: along_z(): return lax.ppermute(a, 'bond', hops)]
    unnamed x17 -> x1, local copies, waits for them, and re-layouts: 9.27 us -> 0.69 us
    pallas_call x9 -> x10, Pallas kernels: 26.7 us -> 29.3 us  [the longest x3 13.6 us: flows(): pl.pallas_call(functools.partial(flow_kernel, dzs, by_plane, not hot), in...]
  transfers between devices with their start and end apart: 35 -> 17, of which waited for: 6 -> 7; matrix products, arithmetic and copies ran while one was open for 0% -> 1% of each run, Pallas kernels for 10% -> 17%
where the time goes in v2:
time: 140 us; the launch traced here: 139 us
  starting transfers between devices  56.4 us (40%)
  waiting for transfers between devices  49.5 us (35%)
  Pallas kernels  30.2 us (22%)
  local copies, waits for them, and re-layouts  2.05 us (1%)
    ppermute x7, waiting for transfers between devices, along_z(): return lax.ppermute(a, 'bond', hops)  33.9 us
    ppermute x6, starting transfers between devices, in_plane(): return lax.ppermute(a, 'bond', [(i, i ^ d) for i in range(bonds)])  32 us
    ppermute x7, starting transfers between devices, along_z(): return lax.ppermute(a, 'bond', hops)  17 us
    ppermute x6, waiting for transfers between devices, in_plane(): return lax.ppermute(a, 'bond', [(i, i ^ d) for i in range(bonds)])  14 us
    pallas_call x3, Pallas kernels, flows(): pl.pallas_call(functools.partial(flow_kernel, dzs, by_plane, not hot), in...  13.6 us
    pallas_call x4, Pallas kernels, place(): pl.pallas_call(functools.partial(place_kernel, units, dzs[0] not in LATE)...  12.5 us
    ppermute x3, starting transfers between devices, along_x(): lax.ppermute(a, 'freq', [(2 * x + y, 2 * ((x + d) % 4) + y) for x in rang...  6.32 us
    pallas_call x1, Pallas kernels, tables(): pl.pallas_call(tables_kernel, in_specs=[SMEM, VMEM, pl.BlockSpec(memory_s...  2.88 us
  transfers between devices with their start and end apart: 17, of which 7 were waited for; matrix products, arithmetic and copies ran while one was open for 1% of the time, Pallas kernels for 17%

profile of v2, /device:TPU:1, one launch (start us, length us, event | category | flops | bytes accessed | tf_op | source)
XLA Modules:
  0.0 139.0 jit_solution(2979688182864922646)
XLA Ops:
  0.7 3.6 %collective-permute-start.1 = (f32[4,2,4,256]{3,2,1,0:T(4,128)S(1)}, f32[4,2,4,256]{3,2,1,0:T(4,128)S(1)}, u32[]{:S(2)}, u32[]{:S(2)}) collective-permute-start(f32[4,2,4,256]{3,2,1,0:T(4,128)S(1)} %get-tuple-element.38), channel_id=1, source_target_pairs={{0,128},{32,160},{64,192},{96,224},{128,0},{160,32},{192,64},{224,... | collective-permute-start | bytes 98312 | tf_op jit(solution)/shard_map/ppermute | solution.py:275
  4.7 2.4 %collective-permute-start.2 = (f32[4,2,4,256]{3,2,1,0:T(4,128)S(1)}, f32[4,2,4,256]{3,2,1,0:T(4,128)S(1)}, u32[]{:S(2)}, u32[]{:S(2)}) collective-permute-start(f32[4,2,4,256]{3,2,1,0:T(4,128)S(1)} %get-tuple-element.38), channel_id=1, source_target_pairs={{0,192},{32,224},{64,0},{96,32},{128,64},{160,96},{192,128},{224,1... | collective-permute-start | bytes 98312 | tf_op jit(solution)/shard_map/ppermute | solution.py:275
  11.9 2.9 %tables.1 = (bf16[2,8,384,384]{3,2,1,0:T(8,128)(2,1)S(1)}, bf16[384,384]{1,0:T(8,128)(2,1)S(1)}, bf16[192,192]{1,0:T(8,128)(2,1)S(1)}) custom-call(s32[4]{0:T(128)S(1)} %compare_select_fusion.2.pos_ref, s32[1,384]{1,0:T(1,128)S(1)} %reshape.9.perm_ref, bf16[2,8,384,384]{3,2,1,0:T(8,128)(2,1)} %bitcast.6), custom_call_target="tpu_custom_call" | custom-call | tf_op jit(solution)/shard_map/tables/pallas_call | solution.py:48
  15.6 2.3 %flow.4 = bf16[4,2,2,48,384]{4,3,2,1,0:T(8,128)(2,1)S(1)} custom-call(s32[4]{0:T(128)S(1)} %compare_select_fusion.2.pos_ref, s32[2,3,3]{2,1,0:T(4,128)S(1)} %copy.10.mask_ref, bf16[2,8,384,384]{3,2,1,0:T(8,128)(2,1)S(1)} %get-tuple-element.23.gamma_ref, f32[16,384]{1,0:T(8,128)S(1)} %bubble.1.bubble_ref), custom_call_target="tpu_custom_call" | custom-call | tf_op jit(solution)/shard_map/flow/pallas_call | solution.py:179
  17.9 7.0 %collective-permute-start.11 = (bf16[4,2,2,48,384]{4,3,2,1,0:T(8,128)(2,1)S(1)}, bf16[4,2,2,48,384]{4,3,2,1,0:T(8,128)(2,1)S(1)}, u32[]{:S(2)}, u32[]{:S(2)}) collective-permute-start(bf16[4,2,2,48,384]{4,3,2,1,0:T(8,128)(2,1)S(1)} %flow.4), channel_id=1, source_target_pairs={{0,16},{1,17},{2,18},{3,19},{4,20},{5,21},{6,22},{7,23},{8,24},{9,... | collective-permute-start | bytes 1769480 | tf_op jit(solution)/shard_map/ppermute | solution.py:292
  24.9 2.9 %flow.5 = (bf16[4,2,2,48,384]{4,3,2,1,0:T(8,128)(2,1)S(1)}, bf16[4,2,2,48,384]{4,3,2,1,0:T(8,128)(2,1)S(1)}) custom-call(s32[4]{0:T(128)S(1)} %compare_select_fusion.2.pos_ref, s32[2,3,3]{2,1,0:T(4,128)S(1)} %copy.10.mask_ref, bf16[2,8,384,384]{3,2,1,0:T(8,128)(2,1)S(1)} %get-tuple-element.23.gamma_ref, f32[16,384]{1,0:T(8,128)S(1)} %bubble.1.bubble_ref), custom_call_target="tpu_custom_call" | custom-call | tf_op jit(solution)/shard_map/flow/pallas_call | solution.py:179
  29.5 2.8 %collective-permute-start.13 = (bf16[4,2,2,48,384]{4,3,2,1,0:T(8,128)(2,1)S(1)}, bf16[4,2,2,48,384]{4,3,2,1,0:T(8,128)(2,1)S(1)}, u32[]{:S(2)}, u32[]{:S(2)}) collective-permute-start(bf16[4,2,2,48,384]{4,3,2,1,0:T(8,128)(2,1)S(1)} %get-tuple-element.33), channel_id=1, source_target_pairs={{0,20},{1,21},{2,22},{3,23},{4,24},{5,25},{6,26},{7,27},{8,28},{9,... | collective-permute-start | bytes 1769480 | tf_op jit(solution)/shard_map/ppermute | solution.py:292
  32.3 8.5 %flow.3 = (bf16[5,2,2,48,384]{4,3,2,1,0:T(8,128)(2,1)S(1)}, bf16[5,2,2,48,384]{4,3,2,1,0:T(8,128)(2,1)S(1)}, bf16[5,2,2,48,384]{4,3,2,1,0:T(8,128)(2,1)S(1)}, bf16[5,2,2,48,384]{4,3,2,1,0:T(8,128)(2,1)S(1)}) custom-call(s32[4]{0:T(128)S(1)} %compare_select_fusion.2.pos_ref, s32[2,3,3]{2,1,0:T(4,128)S(1)} %copy.10.mask_ref, ...), custom_call_target="tpu_custom_call" | custom-call | tf_op jit(solution)/shard_map/flow/pallas_call | solution.py:179
  40.8 3.3 %collective-permute-start.4 = (bf16[5,2,2,48,384]{4,3,2,1,0:T(8,128)(2,1)S(1)}, bf16[5,2,2,48,384]{4,3,2,1,0:T(8,128)(2,1)S(1)}, u32[]{:S(2)}, u32[]{:S(2)}) collective-permute-start(bf16[5,2,2,48,384]{4,3,2,1,0:T(8,128)(2,1)S(1)} %get-tuple-element.25), channel_id=1, source_target_pairs={{0,1},{1,0},{2,3},{3,2},{4,5},{5,4},{6,7},{7,6},{8,9},{9,8},{10,11... | collective-permute-start | bytes 2211848 | tf_op jit(solution)/shard_map/ppermute | solution.py:295
  44.1 2.6 %collective-permute-start.5 = (bf16[5,2,2,48,384]{4,3,2,1,0:T(8,128)(2,1)S(1)}, bf16[5,2,2,48,384]{4,3,2,1,0:T(8,128)(2,1)S(1)}, u32[]{:S(2)}, u32[]{:S(2)}) collective-permute-start(bf16[5,2,2,48,384]{4,3,2,1,0:T(8,128)(2,1)S(1)} %get-tuple-element.26), channel_id=1, source_target_pairs={{0,2},{1,3},{2,0},{3,1},{4,6},{5,7},{6,4},{7,5},{8,10},{9,11},{10,... | collective-permute-start | bytes 2211848 | tf_op jit(solution)/shard_map/ppermute | solution.py:295
  46.7 17.9 %collective-permute-start.6 = (bf16[5,2,2,48,384]{4,3,2,1,0:T(8,128)(2,1)S(1)}, bf16[5,2,2,48,384]{4,3,2,1,0:T(8,128)(2,1)S(1)}, u32[]{:S(2)}, u32[]{:S(2)}) collective-permute-start(bf16[5,2,2,48,384]{4,3,2,1,0:T(8,128)(2,1)S(1)} %get-tuple-element.27), channel_id=1, source_target_pairs={{0,3},{1,2},{2,1},{3,0},{4,7},{5,6},{6,5},{7,4},{8,11},{9,10},{10,... | collective-permute-start | bytes 2211848 | tf_op jit(solution)/shard_map/ppermute | solution.py:295
  64.6 22.8 %collective-permute-done.12.refs_1_ = bf16[4,2,2,48,384]{4,3,2,1,0:T(8,128)(2,1)S(1)} collective-permute-done((bf16[4,2,2,48,384]{4,3,2,1,0:T(8,128)(2,1)S(1)}, bf16[4,2,2,48,384]{4,3,2,1,0:T(8,128)(2,1)S(1)}, u32[]{:S(2)}, u32[]{:S(2)}) %collective-permute-start.12) | collective-permute-done | bytes 589856 | tf_op jit(solution)/shard_map/ppermute | solution.py:292
  88.4 2.1 %collective-permute-start.14 = (bf16[3,2,2,48,384]{4,3,2,1,0:T(8,128)(2,1)S(1)}, bf16[3,2,2,48,384]{4,3,2,1,0:T(8,128)(2,1)S(1)}, u32[]{:S(2)}, u32[]{:S(2)}) collective-permute-start(bf16[3,2,2,48,384]{4,3,2,1,0:T(8,128)(2,1)S(1)} %get-tuple-element.34), channel_id=1, source_target_pairs={{0,1},{1,0},{2,3},{3,2},{4,5},{5,4},{6,7},{7,6},{8,9},{9,8},{10,11... | collective-permute-start | bytes 1327112 | tf_op jit(solution)/shard_map/ppermute | solution.py:295
  90.5 2.6 %collective-permute-start.15 = (bf16[3,2,2,48,384]{4,3,2,1,0:T(8,128)(2,1)S(1)}, bf16[3,2,2,48,384]{4,3,2,1,0:T(8,128)(2,1)S(1)}, u32[]{:S(2)}, u32[]{:S(2)}) collective-permute-start(bf16[3,2,2,48,384]{4,3,2,1,0:T(8,128)(2,1)S(1)} %get-tuple-element.35), channel_id=1, source_target_pairs={{0,2},{1,3},{2,0},{3,1},{4,6},{5,7},{6,4},{7,5},{8,10},{9,11},{10,... | collective-permute-start | bytes 1327112 | tf_op jit(solution)/shard_map/ppermute | solution.py:295
  93.5 2.4 %collective-permute-start.9 = (bf16[4,2,2,48,384]{4,3,2,1,0:T(8,128)(2,1)S(1)}, bf16[4,2,2,48,384]{4,3,2,1,0:T(8,128)(2,1)S(1)}, u32[]{:S(2)}, u32[]{:S(2)}) collective-permute-start(bf16[4,2,2,48,384]{4,3,2,1,0:T(8,128)(2,1)S(1)} %get-tuple-element.30), channel_id=1, source_target_pairs={{0,8},{1,9},{2,10},{3,11},{4,12},{5,13},{6,14},{7,15},{8,16},{9,17... | collective-permute-start | bytes 1769480 | tf_op jit(solution)/shard_map/ppermute | solution.py:292
  98.8 4.8 %collective-permute-done.15.refs_4_ = bf16[3,2,2,48,384]{4,3,2,1,0:T(8,128)(2,1)S(1)} collective-permute-done((bf16[3,2,2,48,384]{4,3,2,1,0:T(8,128)(2,1)S(1)}, bf16[3,2,2,48,384]{4,3,2,1,0:T(8,128)(2,1)S(1)}, u32[]{:S(2)}, u32[]{:S(2)}) %collective-permute-start.15) | collective-permute-done | bytes 442400 | tf_op jit(solution)/shard_map/ppermute | solution.py:295
  103.6 3.5 %collective-permute-start.16 = (bf16[3,2,2,48,384]{4,3,2,1,0:T(8,128)(2,1)S(1)}, bf16[3,2,2,48,384]{4,3,2,1,0:T(8,128)(2,1)S(1)}, u32[]{:S(2)}, u32[]{:S(2)}) collective-permute-start(bf16[3,2,2,48,384]{4,3,2,1,0:T(8,128)(2,1)S(1)} %get-tuple-element.36), channel_id=1, source_target_pairs={{0,3},{1,2},{2,1},{3,0},{4,7},{5,6},{6,5},{7,4},{8,11},{9,10},{10,... | collective-permute-start | bytes 1327112 | tf_op jit(solution)/shard_map/ppermute | solution.py:295
  107.1 1.8 %place.4.refs_6_ = bf16[2,2,12,128,384]{4,3,2,1,0:T(8,128)(2,1)} custom-call(s32[4]{0:T(128)S(1)} %compare_select_fusion.2.pos_ref, bf16[384,384]{1,0:T(8,128)(2,1)S(1)} %get-tuple-element.21.refs_0_.hot_ref, bf16[192,192]{1,0:T(8,128)(2,1)S(1)} %get-tuple-element.22.rows_ref, bf16[5,2,2,48,384]{4,3,2,1,0:T(8,128)(2,1)S(1)} %get-tuple-element.24.refs_0_, ...), custom_call_target="tpu_custom_call" | custom-call | tf_op jit(solution)/shard_map/place/pallas_call | solution.py:246
  108.9 9.1 %collective-permute-done.16.refs_5_ = bf16[3,2,2,48,384]{4,3,2,1,0:T(8,128)(2,1)S(1)} collective-permute-done((bf16[3,2,2,48,384]{4,3,2,1,0:T(8,128)(2,1)S(1)}, bf16[3,2,2,48,384]{4,3,2,1,0:T(8,128)(2,1)S(1)}, u32[]{:S(2)}, u32[]{:S(2)}) %collective-permute-start.16) | collective-permute-done | bytes 442400 | tf_op jit(solution)/shard_map/ppermute | solution.py:295
  118.1 4.9 %place.5.refs_2_ = bf16[2,2,12,128,384]{4,3,2,1,0:T(8,128)(2,1)} custom-call(s32[4]{0:T(128)S(1)} %compare_select_fusion.2.pos_ref, bf16[384,384]{1,0:T(8,128)(2,1)S(1)} %get-tuple-element.21.refs_0_.hot_ref, bf16[192,192]{1,0:T(8,128)(2,1)S(1)} %get-tuple-element.22.rows_ref, ...), custom_call_target="tpu_custom_call", output_to_operand_aliasing={{}: (9, {})} | custom-call | tf_op jit(solution)/shard_map/place/pallas_call | solution.py:246
  122.9 5.5 %collective-permute-done.9.refs_0_ = bf16[4,2,2,48,384]{4,3,2,1,0:T(8,128)(2,1)S(1)} collective-permute-done((bf16[4,2,2,48,384]{4,3,2,1,0:T(8,128)(2,1)S(1)}, bf16[4,2,2,48,384]{4,3,2,1,0:T(8,128)(2,1)S(1)}, u32[]{:S(2)}, u32[]{:S(2)}) %collective-permute-start.9) | collective-permute-done | bytes 589856 | tf_op jit(solution)/shard_map/ppermute | solution.py:292
  128.5 2.9 %place.6.refs_2_ = bf16[2,2,12,128,384]{4,3,2,1,0:T(8,128)(2,1)} custom-call(s32[4]{0:T(128)S(1)} %compare_select_fusion.2.pos_ref, bf16[384,384]{1,0:T(8,128)(2,1)S(1)} %get-tuple-element.21.refs_0_.hot_ref, bf16[192,192]{1,0:T(8,128)(2,1)S(1)} %get-tuple-element.22.rows_ref, ...), custom_call_target="tpu_custom_call", output_to_operand_aliasing={{}: (5, {})} | custom-call | tf_op jit(solution)/shard_map/place/pallas_call | solution.py:246
  131.4 4.7 %collective-permute-done.8.refs_1_ = bf16[4,2,2,48,384]{4,3,2,1,0:T(8,128)(2,1)S(1)} collective-permute-done((bf16[4,2,2,48,384]{4,3,2,1,0:T(8,128)(2,1)S(1)}, bf16[4,2,2,48,384]{4,3,2,1,0:T(8,128)(2,1)S(1)}, u32[]{:S(2)}, u32[]{:S(2)}) %collective-permute-start.8) | collective-permute-done | bytes 589856 | tf_op jit(solution)/shard_map/ppermute | solution.py:292
  136.1 2.9 %place.7 = bf16[2,2,12,128,384]{4,3,2,1,0:T(8,128)(2,1)} custom-call(s32[4]{0:T(128)S(1)} %compare_select_fusion.2.pos_ref, bf16[384,384]{1,0:T(8,128)(2,1)S(1)} %get-tuple-element.21.refs_0_.hot_ref, bf16[192,192]{1,0:T(8,128)(2,1)S(1)} %get-tuple-element.22.rows_ref, ...), custom_call_target="tpu_custom_call", output_to_operand_aliasing={{}: (5, {})} | custom-call | tf_op jit(solution)/shard_map/place/pallas_call | solution.py:246
  (27 shorter events, 12.6 us)
Async XLA Ops:
  0.7 6.3 %collective-permute-start.1 = (f32[4,2,4,256]{3,2,1,0:T(4,128)S(1)}, f32[4,2,4,256]{3,2,1,0:T(4,128)S(1)}, u32[]{:S(2)}, u32[]{:S(2)}) collective-permute-start(f32[4,2,4,256]{3,2,1,0:T(4,128)S(1)} %get-tuple-element.38), channel_id=1, source_target_pairs={{0,128},{32,160},{64,192},{96,224},{128,0},{160,32},{192,64},{224,... | collective-permute-start | bytes 98312 | tf_op jit(solution)/shard_map/ppermute | solution.py:275
  4.4 4.3 %collective-permute-start = (f32[4,2,4,256]{3,2,1,0:T(4,128)S(1)}, f32[4,2,4,256]{3,2,1,0:T(4,128)S(1)}, u32[]{:S(2)}, u32[]{:S(2)}) collective-permute-start(f32[4,2,4,256]{3,2,1,0:T(4,128)S(1)} %get-tuple-element.38), channel_id=1, source_target_pairs={{0,64},{32,96},{64,128},{96,160},{128,192},{160,224},{192,0},{224,... | collective-permute-start | bytes 98312 | tf_op jit(solution)/shard_map/ppermute | solution.py:275
  4.7 4.0 %collective-permute-start.2 = (f32[4,2,4,256]{3,2,1,0:T(4,128)S(1)}, f32[4,2,4,256]{3,2,1,0:T(4,128)S(1)}, u32[]{:S(2)}, u32[]{:S(2)}) collective-permute-start(f32[4,2,4,256]{3,2,1,0:T(4,128)S(1)} %get-tuple-element.38), channel_id=1, source_target_pairs={{0,192},{32,224},{64,0},{96,32},{128,64},{160,96},{192,128},{224,1... | collective-permute-start | bytes 98312 | tf_op jit(solution)/shard_map/ppermute | solution.py:275
  8.7 6.0 %collective-permute-start.3 = (f32[4,4,2,4,256]{4,3,2,1,0:T(4,128)S(1)}, f32[4,4,2,4,256]{4,3,2,1,0:T(4,128)S(1)}, u32[]{:S(2)}, u32[]{:S(2)}) collective-permute-start(f32[4,4,2,4,256]{4,3,2,1,0:T(4,128)S(1)} %pad_maximum_fusion.mine_ref), channel_id=1, source_target_pairs={{0,32},{32,0},{64,96},{96,64},{128,160},{160,128},{192,224},{224,1... | collective-permute-start | bytes 393224 | tf_op jit(solution)/shard_map/ppermute | solution.py:282
  17.9 28.8 %collective-permute-start.11 = (bf16[4,2,2,48,384]{4,3,2,1,0:T(8,128)(2,1)S(1)}, bf16[4,2,2,48,384]{4,3,2,1,0:T(8,128)(2,1)S(1)}, u32[]{:S(2)}, u32[]{:S(2)}) collective-permute-start(bf16[4,2,2,48,384]{4,3,2,1,0:T(8,128)(2,1)S(1)} %flow.4), channel_id=1, source_target_pairs={{0,16},{1,17},{2,18},{3,19},{4,20},{5,21},{6,22},{7,23},{8,24},{9,... | collective-permute-start | bytes 1769480 | tf_op jit(solution)/shard_map/ppermute | solution.py:292
  27.7 59.7 %collective-permute-start.12 = (bf16[4,2,2,48,384]{4,3,2,1,0:T(8,128)(2,1)S(1)}, bf16[4,2,2,48,384]{4,3,2,1,0:T(8,128)(2,1)S(1)}, u32[]{:S(2)}, u32[]{:S(2)}) collective-permute-start(bf16[4,2,2,48,384]{4,3,2,1,0:T(8,128)(2,1)S(1)} %get-tuple-element.32), channel_id=1, source_target_pairs={{0,12},{1,13},{2,14},{3,15},{4,16},{5,17},{6,18},{7,19},{8,20},{9,... | collective-permute-start | bytes 1769480 | tf_op jit(solution)/shard_map/ppermute | solution.py:292
  29.5 58.8 %collective-permute-start.13 = (bf16[4,2,2,48,384]{4,3,2,1,0:T(8,128)(2,1)S(1)}, bf16[4,2,2,48,384]{4,3,2,1,0:T(8,128)(2,1)S(1)}, u32[]{:S(2)}, u32[]{:S(2)}) collective-permute-start(bf16[4,2,2,48,384]{4,3,2,1,0:T(8,128)(2,1)S(1)} %get-tuple-element.33), channel_id=1, source_target_pairs={{0,20},{1,21},{2,22},{3,23},{4,24},{5,25},{6,26},{7,27},{8,28},{9,... | collective-permute-start | bytes 1769480 | tf_op jit(solution)/shard_map/ppermute | solution.py:292
  40.8 52.4 %collective-permute-start.4 = (bf16[5,2,2,48,384]{4,3,2,1,0:T(8,128)(2,1)S(1)}, bf16[5,2,2,48,384]{4,3,2,1,0:T(8,128)(2,1)S(1)}, u32[]{:S(2)}, u32[]{:S(2)}) collective-permute-start(bf16[5,2,2,48,384]{4,3,2,1,0:T(8,128)(2,1)S(1)} %get-tuple-element.25), channel_id=1, source_target_pairs={{0,1},{1,0},{2,3},{3,2},{4,5},{5,4},{6,7},{7,6},{8,9},{9,8},{10,11... | collective-permute-start | bytes 2211848 | tf_op jit(solution)/shard_map/ppermute | solution.py:295
  44.1 49.1 %collective-permute-start.5 = (bf16[5,2,2,48,384]{4,3,2,1,0:T(8,128)(2,1)S(1)}, bf16[5,2,2,48,384]{4,3,2,1,0:T(8,128)(2,1)S(1)}, u32[]{:S(2)}, u32[]{:S(2)}) collective-permute-start(bf16[5,2,2,48,384]{4,3,2,1,0:T(8,128)(2,1)S(1)} %get-tuple-element.26), channel_id=1, source_target_pairs={{0,2},{1,3},{2,0},{3,1},{4,6},{5,7},{6,4},{7,5},{8,10},{9,11},{10,... | collective-permute-start | bytes 2211848 | tf_op jit(solution)/shard_map/ppermute | solution.py:295
  46.7 46.4 %collective-permute-start.6 = (bf16[5,2,2,48,384]{4,3,2,1,0:T(8,128)(2,1)S(1)}, bf16[5,2,2,48,384]{4,3,2,1,0:T(8,128)(2,1)S(1)}, u32[]{:S(2)}, u32[]{:S(2)}) collective-permute-start(bf16[5,2,2,48,384]{4,3,2,1,0:T(8,128)(2,1)S(1)} %get-tuple-element.27), channel_id=1, source_target_pairs={{0,3},{1,2},{2,1},{3,0},{4,7},{5,6},{6,5},{7,4},{8,11},{9,10},{10,... | collective-permute-start | bytes 2211848 | tf_op jit(solution)/shard_map/ppermute | solution.py:295
  88.4 9.1 %collective-permute-start.14 = (bf16[3,2,2,48,384]{4,3,2,1,0:T(8,128)(2,1)S(1)}, bf16[3,2,2,48,384]{4,3,2,1,0:T(8,128)(2,1)S(1)}, u32[]{:S(2)}, u32[]{:S(2)}) collective-permute-start(bf16[3,2,2,48,384]{4,3,2,1,0:T(8,128)(2,1)S(1)} %get-tuple-element.34), channel_id=1, source_target_pairs={{0,1},{1,0},{2,3},{3,2},{4,5},{5,4},{6,7},{7,6},{8,9},{9,8},{10,11... | collective-permute-start | bytes 1327112 | tf_op jit(solution)/shard_map/ppermute | solution.py:295
  90.5 13.1 %collective-permute-start.15 = (bf16[3,2,2,48,384]{4,3,2,1,0:T(8,128)(2,1)S(1)}, bf16[3,2,2,48,384]{4,3,2,1,0:T(8,128)(2,1)S(1)}, u32[]{:S(2)}, u32[]{:S(2)}) collective-permute-start(bf16[3,2,2,48,384]{4,3,2,1,0:T(8,128)(2,1)S(1)} %get-tuple-element.35), channel_id=1, source_target_pairs={{0,2},{1,3},{2,0},{3,1},{4,6},{5,7},{6,4},{7,5},{8,10},{9,11},{10,... | collective-permute-start | bytes 1327112 | tf_op jit(solution)/shard_map/ppermute | solution.py:295
  93.4 38.0 %collective-permute-start.7 = (bf16[4,2,2,48,384]{4,3,2,1,0:T(8,128)(2,1)S(1)}, bf16[4,2,2,48,384]{4,3,2,1,0:T(8,128)(2,1)S(1)}, u32[]{:S(2)}, u32[]{:S(2)}) collective-permute-start(bf16[4,2,2,48,384]{4,3,2,1,0:T(8,128)(2,1)S(1)} %get-tuple-element.28), channel_id=1, source_target_pairs={{0,4},{1,5},{2,6},{3,7},{4,8},{5,9},{6,10},{7,11},{8,12},{9,13},{1... | collective-permute-start | bytes 1769480 | tf_op jit(solution)/shard_map/ppermute | solution.py:292
  93.5 35.0 %collective-permute-start.9 = (bf16[4,2,2,48,384]{4,3,2,1,0:T(8,128)(2,1)S(1)}, bf16[4,2,2,48,384]{4,3,2,1,0:T(8,128)(2,1)S(1)}, u32[]{:S(2)}, u32[]{:S(2)}) collective-permute-start(bf16[4,2,2,48,384]{4,3,2,1,0:T(8,128)(2,1)S(1)} %get-tuple-element.30), channel_id=1, source_target_pairs={{0,8},{1,9},{2,10},{3,11},{4,12},{5,13},{6,14},{7,15},{8,16},{9,17... | collective-permute-start | bytes 1769480 | tf_op jit(solution)/shard_map/ppermute | solution.py:292
  95.9 32.6 %collective-permute-start.10 = (bf16[4,2,2,48,384]{4,3,2,1,0:T(8,128)(2,1)S(1)}, bf16[4,2,2,48,384]{4,3,2,1,0:T(8,128)(2,1)S(1)}, u32[]{:S(2)}, u32[]{:S(2)}) collective-permute-start(bf16[4,2,2,48,384]{4,3,2,1,0:T(8,128)(2,1)S(1)} %get-tuple-element.31), channel_id=1, source_target_pairs={{0,24},{1,25},{2,26},{3,27},{4,28},{5,29},{6,30},{7,31},{8,0},{9,1... | collective-permute-start | bytes 1769480 | tf_op jit(solution)/shard_map/ppermute | solution.py:292
  97.5 38.5 %collective-permute-start.8 = (bf16[4,2,2,48,384]{4,3,2,1,0:T(8,128)(2,1)S(1)}, bf16[4,2,2,48,384]{4,3,2,1,0:T(8,128)(2,1)S(1)}, u32[]{:S(2)}, u32[]{:S(2)}) collective-permute-start(bf16[4,2,2,48,384]{4,3,2,1,0:T(8,128)(2,1)S(1)} %get-tuple-element.29), channel_id=1, source_target_pairs={{0,28},{1,29},{2,30},{3,31},{4,0},{5,1},{6,2},{7,3},{8,4},{9,5},{1... | collective-permute-start | bytes 1769480 | tf_op jit(solution)/shard_map/ppermute | solution.py:292
  103.6 14.4 %collective-permute-start.16 = (bf16[3,2,2,48,384]{4,3,2,1,0:T(8,128)(2,1)S(1)}, bf16[3,2,2,48,384]{4,3,2,1,0:T(8,128)(2,1)S(1)}, u32[]{:S(2)}, u32[]{:S(2)}) collective-permute-start(bf16[3,2,2,48,384]{4,3,2,1,0:T(8,128)(2,1)S(1)} %get-tuple-element.36), channel_id=1, source_target_pairs={{0,3},{1,2},{2,1},{3,0},{4,7},{5,6},{6,5},{7,4},{8,11},{9,10},{10,... | collective-permute-start | bytes 1327112 | tf_op jit(solution)/shard_map/ppermute | solution.py:295

commit v3 on v2

--- a/solution.py
+++ b/solution.py
@@ -144,12 +144,14 @@
             l_real = (g_real * b_real - g_imag * b_imag).astype(jnp.bfloat16)
             l_imag = (g_real * b_imag + g_imag * b_real).astype(jnp.bfloat16)
             dot = functools.partial(jnp.dot, preferred_element_type=jnp.float32)
-            real = dot(l_real, gamma_ref[0, i]) - dot(l_imag, gamma_ref[1, i])
-            imag = dot(l_real, gamma_ref[1, i]) + dot(l_imag, gamma_ref[0, i])
-            values = [jnp.where(mask, value, 0.0) for value in (real, imag)]
+            left = jnp.concatenate([l_real, l_imag], axis=0)
+            by_real, by_imag = dot(left, gamma_ref[0, i]), dot(left, gamma_ref[1, i])
+            cut = planes * height
+            values = [by_real[:cut] - by_imag[cut:], by_imag[:cut] + by_real[cut:]]
+            values = [jnp.where(mask, value, 0.0) for value in values]
             if hot_ref is not None:
                 both = dot(jnp.concatenate(values, axis=0).astype(jnp.bfloat16), hot_ref[...])
-                values = [both[: planes * height], both[planes * height :]]
+                values = [both[:cut], both[cut:]]
             for part, value in enumerate(values):
                 for j in range(planes):
                     for p in range(PLANE):
@@ -207,6 +209,56 @@
     )(*arrays)
 
 
+def order_kernel(rows_ref, *refs):
+    ins, outs = refs[:PLANE], refs[PLANE:]
+    for b, out in enumerate(outs):
+        for part in range(2):
+            for w in range(2):
+                rows = jnp.concatenate([ref[b, part, w] for ref in ins], axis=0)
+                rows = jnp.dot(rows_ref[...], rows, preferred_element_type=jnp.float32)
+                out[part, w] = rows.astype(jnp.bfloat16).reshape(out.shape[2:])
+
+
+def order_rows(rows, arrays):
+    number, _, wide, height, order = arrays[0].shape
+    shape = jax.ShapeDtypeStruct((2, wide, height // PLANE, 16, order), jnp.bfloat16)
+    return pl.pallas_call(
+        order_kernel,
+        in_specs=[VMEM] * (1 + PLANE),
+        out_specs=[VMEM] * (number - 1),
+        out_shape=[shape] * (number - 1),
+        compiler_params=params(),
+        name="order_rows",
+    )(rows, *arrays)
+
+
+def deliver_kernel(dzs, pos_ref, *refs):
+    out_ref, sems = refs[-2:]
+    copies = []
+    for j, dz in enumerate(dzs):
+        at = pl.multiple_of(((pos_ref[1] + 8 - dz) & 7) * 16, 16)
+        for part in range(2):
+            to = out_ref.at[part, :, :, pl.ds(at, 16), :]
+            copies.append(pltpu.make_async_copy(refs[j].at[part], to, sems.at[2 * j + part]))
+    for copy in copies:
+        copy.start()
+    for copy in copies:
+        copy.wait()
+
+
+def deliver(pos, arrays, so_far, dzs):
+    return pl.pallas_call(
+        functools.partial(deliver_kernel, dzs),
+        in_specs=[SMEM] + [VMEM] * len(arrays) + [pl.BlockSpec(memory_space=pl.ANY)],
+        out_specs=pl.BlockSpec(memory_space=pl.ANY),
+        out_shape=jax.ShapeDtypeStruct(so_far.shape, so_far.dtype),
+        scratch_shapes=[pltpu.SemaphoreType.DMA((2 * len(arrays),))],
+        input_output_aliases={1 + len(arrays): 0},
+        compiler_params=params(),
+        name="deliver",
+    )(pos, *arrays, so_far)
+
+
 def place_kernel(units, columns, pos_ref, hot_ref, rows_ref, *refs):
     out_ref, wide = refs[-2:]
     height, _ = refs[0].shape[3:]
@@ -301,7 +353,7 @@
         early += [along_z(a, dz) for a, dz in zip(bundles, dzs)]
     sets = flow(LATE, False, ones[0])
     sets = [sets[0]] + [in_plane(sets[d], d) for d in range(1, PLANE)]
-    bundles = turn(sets, range(len(LATE) - 1))
+    bundles = order_rows(ones[1], sets)
     late = [along_z(a, dz) for a, dz in zip(bundles, LATE)]
     back = turn(early, range(1, PLANE))
     back = [in_plane(a, d) for d, a in enumerate(back, 1)]
@@ -310,11 +362,10 @@
     last = len(LATE) - 1
     put = functools.partial(place, pos, ones)
     out = put(sets, [[(d, last) for d in range(PLANE)]], None, shape, LATE[last:])
+    out = deliver(pos, late[:2], out, LATE[:2])
     units = [[(j, 0)] + [(len(early) + d, j) for d in range(PLANE - 1)] for j in range(len(early))]
     out = put(early + back, units, out, shape, HALF + FAR)
-    units = [[(j % 2, d) for d in range(PLANE)] for j in range(last)]
-    out = put(late[:2], units[:2], out, shape, LATE[:2])
-    return put(late[2:], units[2:], out, shape, LATE[2:last])
+    return deliver(pos, late[2:], out, LATE[2:last])
 
 
 def solution(mesh):

time: 140 us -> 157 us (1.12)
  the two profiles are of different devices: /device:TPU:1 before, /device:TPU:39 now
where the time goes in v3:
time: 157 us
  waiting for transfers between devices  87.5 us (56%)
  starting transfers between devices  38.2 us (24%)
  Pallas kernels  28 us (18%)
  local copies, waits for them, and re-layouts  2.05 us (1%)
    ppermute x7, waiting for transfers between devices, along_z(): return lax.ppermute(a, 'bond', hops)  50.2 us
    ppermute x6, waiting for transfers between devices, in_plane(): return lax.ppermute(a, 'bond', [(i, i ^ d) for i in range(bonds)])  33.3 us
    ppermute x7, starting transfers between devices, along_z(): return lax.ppermute(a, 'bond', hops)  22.6 us
    pallas_call x3, Pallas kernels, flows(): pl.pallas_call(functools.partial(flow_kernel, dzs, by_plane, not hot), in...  13.3 us
    ppermute x6, starting transfers between devices, in_plane(): return lax.ppermute(a, 'bond', [(i, i ^ d) for i in range(bonds)])  11.1 us
    pallas_call x2, Pallas kernels, place(): pl.pallas_call(functools.partial(place_kernel, units, dzs[0] not in LATE)...  6.68 us
    ppermute x3, waiting for transfers between devices, along_x(): lax.ppermute(a, 'freq', [(2 * x + y, 2 * ((x + d) % 4) + y) for x in rang...  3.97 us
    pallas_call x2, Pallas kernels, deliver(): pl.pallas_call(functools.partial(deliver_kernel, dzs), in_specs=[SMEM] +...  3.17 us
  transfers between devices with their start and end apart: 17, of which 8 were waited for; matrix products, arithmetic and copies ran while one was open for 1% of the time, Pallas kernels for 11%

profile of v3, /device:TPU:39, one launch (start us, length us, event | category | flops | bytes accessed | tf_op | source)
XLA Modules:
  0.0 156.8 jit_solution(10218607941735057006)
XLA Ops:
  2.0 1.8 %collective-permute-start = (f32[4,2,4,256]{3,2,1,0:T(4,128)S(1)}, f32[4,2,4,256]{3,2,1,0:T(4,128)S(1)}, u32[]{:S(2)}, u32[]{:S(2)}) collective-permute-start(f32[4,2,4,256]{3,2,1,0:T(4,128)S(1)} %get-tuple-element.38), channel_id=1, source_target_pairs={{0,64},{32,96},{64,128},{96,160},{128,192},{160,224},{192,0},{224,... | collective-permute-start | bytes 98312 | tf_op jit(solution)/shard_map/ppermute | solution.py:327
  5.1 2.6 %collective-permute-done.2 = f32[4,2,4,256]{3,2,1,0:T(4,128)S(1)} collective-permute-done((f32[4,2,4,256]{3,2,1,0:T(4,128)S(1)}, f32[4,2,4,256]{3,2,1,0:T(4,128)S(1)}, u32[]{:S(2)}, u32[]{:S(2)}) %collective-permute-start.2) | collective-permute-done | bytes 32800 | tf_op jit(solution)/shard_map/ppermute | solution.py:327
  11.2 2.9 %tables.1 = (bf16[2,8,384,384]{3,2,1,0:T(8,128)(2,1)S(1)}, bf16[384,384]{1,0:T(8,128)(2,1)S(1)}, bf16[192,192]{1,0:T(8,128)(2,1)S(1)}) custom-call(s32[4]{0:T(128)S(1)} %compare_select_fusion.2.pos_ref, s32[1,384]{1,0:T(1,128)S(1)} %reshape.9.perm_ref, bf16[2,8,384,384]{3,2,1,0:T(8,128)(2,1)} %bitcast.6), custom_call_target="tpu_custom_call" | custom-call | tf_op jit(solution)/shard_map/tables/pallas_call | solution.py:48
  15.0 9.0 %flow.3 = (bf16[5,2,2,48,384]{4,3,2,1,0:T(8,128)(2,1)S(1)}, bf16[5,2,2,48,384]{4,3,2,1,0:T(8,128)(2,1)S(1)}, bf16[5,2,2,48,384]{4,3,2,1,0:T(8,128)(2,1)S(1)}, bf16[5,2,2,48,384]{4,3,2,1,0:T(8,128)(2,1)S(1)}) custom-call(s32[4]{0:T(128)S(1)} %compare_select_fusion.2.pos_ref, s32[2,3,3]{2,1,0:T(4,128)S(1)} %copy.10.mask_ref, ...), custom_call_target="tpu_custom_call" | custom-call | tf_op jit(solution)/shard_map/flow/pallas_call | solution.py:181
  24.0 2.7 %collective-permute-start.4 = (bf16[5,2,2,48,384]{4,3,2,1,0:T(8,128)(2,1)S(1)}, bf16[5,2,2,48,384]{4,3,2,1,0:T(8,128)(2,1)S(1)}, u32[]{:S(2)}, u32[]{:S(2)}) collective-permute-start(bf16[5,2,2,48,384]{4,3,2,1,0:T(8,128)(2,1)S(1)} %get-tuple-element.25), channel_id=1, source_target_pairs={{0,1},{1,0},{2,3},{3,2},{4,5},{5,4},{6,7},{7,6},{8,9},{9,8},{10,11... | collective-permute-start | bytes 2211848 | tf_op jit(solution)/shard_map/ppermute | solution.py:347
  26.7 2.6 %collective-permute-start.5 = (bf16[5,2,2,48,384]{4,3,2,1,0:T(8,128)(2,1)S(1)}, bf16[5,2,2,48,384]{4,3,2,1,0:T(8,128)(2,1)S(1)}, u32[]{:S(2)}, u32[]{:S(2)}) collective-permute-start(bf16[5,2,2,48,384]{4,3,2,1,0:T(8,128)(2,1)S(1)} %get-tuple-element.26), channel_id=1, source_target_pairs={{0,2},{1,3},{2,0},{3,1},{4,6},{5,7},{6,4},{7,5},{8,10},{9,11},{10,... | collective-permute-start | bytes 2211848 | tf_op jit(solution)/shard_map/ppermute | solution.py:347
  30.0 1.8 %flow.4 = bf16[4,2,2,48,384]{4,3,2,1,0:T(8,128)(2,1)S(1)} custom-call(s32[4]{0:T(128)S(1)} %compare_select_fusion.2.pos_ref, s32[2,3,3]{2,1,0:T(4,128)S(1)} %copy.10.mask_ref, bf16[2,8,384,384]{3,2,1,0:T(8,128)(2,1)S(1)} %get-tuple-element.22.gamma_ref, f32[16,384]{1,0:T(8,128)S(1)} %bubble.1.bubble_ref), custom_call_target="tpu_custom_call" | custom-call | tf_op jit(solution)/shard_map/flow/pallas_call | solution.py:181
  31.7 6.1 %collective-permute-start.9 = (bf16[4,2,2,48,384]{4,3,2,1,0:T(8,128)(2,1)S(1)}, bf16[4,2,2,48,384]{4,3,2,1,0:T(8,128)(2,1)S(1)}, u32[]{:S(2)}, u32[]{:S(2)}) collective-permute-start(bf16[4,2,2,48,384]{4,3,2,1,0:T(8,128)(2,1)S(1)} %flow.4), channel_id=1, source_target_pairs={{0,16},{1,17},{2,18},{3,19},{4,20},{5,21},{6,22},{7,23},{8,24},{9,... | collective-permute-start | bytes 1769480 | tf_op jit(solution)/shard_map/ppermute | solution.py:344
  37.9 2.5 %flow.5 = (bf16[4,2,2,48,384]{4,3,2,1,0:T(8,128)(2,1)S(1)}, bf16[4,2,2,48,384]{4,3,2,1,0:T(8,128)(2,1)S(1)}) custom-call(s32[4]{0:T(128)S(1)} %compare_select_fusion.2.pos_ref, s32[2,3,3]{2,1,0:T(4,128)S(1)} %copy.10.mask_ref, bf16[2,8,384,384]{3,2,1,0:T(8,128)(2,1)S(1)} %get-tuple-element.22.gamma_ref, f32[16,384]{1,0:T(8,128)S(1)} %bubble.1.bubble_ref), custom_call_target="tpu_custom_call" | custom-call | tf_op jit(solution)/shard_map/flow/pallas_call | solution.py:181
  40.5 4.5 %collective-permute-start.11 = (bf16[4,2,2,48,384]{4,3,2,1,0:T(8,128)(2,1)S(1)}, bf16[4,2,2,48,384]{4,3,2,1,0:T(8,128)(2,1)S(1)}, u32[]{:S(2)}, u32[]{:S(2)}) collective-permute-start(bf16[4,2,2,48,384]{4,3,2,1,0:T(8,128)(2,1)S(1)} %get-tuple-element.31), channel_id=1, source_target_pairs={{0,20},{1,21},{2,22},{3,23},{4,24},{5,25},{6,26},{7,27},{8,28},{9,... | collective-permute-start | bytes 1769480 | tf_op jit(solution)/shard_map/ppermute | solution.py:344
  46.2 16.4 %collective-permute-done.6.refs_3_ = bf16[5,2,2,48,384]{4,3,2,1,0:T(8,128)(2,1)S(1)} collective-permute-done((bf16[5,2,2,48,384]{4,3,2,1,0:T(8,128)(2,1)S(1)}, bf16[5,2,2,48,384]{4,3,2,1,0:T(8,128)(2,1)S(1)}, u32[]{:S(2)}, u32[]{:S(2)}) %collective-permute-start.6) | collective-permute-done | bytes 737312 | tf_op jit(solution)/shard_map/ppermute | solution.py:347
  63.5 3.1 %collective-permute-start.15 = (bf16[2,2,12,16,384]{4,3,2,1,0:T(8,128)(2,1)S(1)}, bf16[2,2,12,16,384]{4,3,2,1,0:T(8,128)(2,1)S(1)}, u32[]{:S(2)}, u32[]{:S(2)}) collective-permute-start(bf16[2,2,12,16,384]{4,3,2,1,0:T(8,128)(2,1)S(1)} %get-tuple-element.35), channel_id=1, source_target_pairs={{0,8},{1,9},{2,10},{3,11},{4,12},{5,13},{6,14},{7,15},{8,16},{9,17... | collective-permute-start | bytes 1769480 | tf_op jit(solution)/shard_map/ppermute | solution.py:344
  66.6 2.2 %collective-permute-start.16 = (bf16[2,2,12,16,384]{4,3,2,1,0:T(8,128)(2,1)S(1)}, bf16[2,2,12,16,384]{4,3,2,1,0:T(8,128)(2,1)S(1)}, u32[]{:S(2)}, u32[]{:S(2)}) collective-permute-start(bf16[2,2,12,16,384]{4,3,2,1,0:T(8,128)(2,1)S(1)} %get-tuple-element.36), channel_id=1, source_target_pairs={{0,24},{1,25},{2,26},{3,27},{4,28},{5,29},{6,30},{7,31},{8,0},{9,1... | collective-permute-start | bytes 1769480 | tf_op jit(solution)/shard_map/ppermute | solution.py:344
  69.5 31.9 %collective-permute-done.10.refs_1_ = bf16[4,2,2,48,384]{4,3,2,1,0:T(8,128)(2,1)S(1)} collective-permute-done((bf16[4,2,2,48,384]{4,3,2,1,0:T(8,128)(2,1)S(1)}, bf16[4,2,2,48,384]{4,3,2,1,0:T(8,128)(2,1)S(1)}, u32[]{:S(2)}, u32[]{:S(2)}) %collective-permute-start.10) | collective-permute-done | bytes 589856 | tf_op jit(solution)/shard_map/ppermute | solution.py:344
  101.4 6.1 %collective-permute-start.8 = (bf16[2,2,12,16,384]{4,3,2,1,0:T(8,128)(2,1)S(1)}, bf16[2,2,12,16,384]{4,3,2,1,0:T(8,128)(2,1)S(1)}, u32[]{:S(2)}, u32[]{:S(2)}) collective-permute-start(bf16[2,2,12,16,384]{4,3,2,1,0:T(8,128)(2,1)S(1)} %get-tuple-element.29), channel_id=1, source_target_pairs={{0,28},{1,29},{2,30},{3,31},{4,0},{5,1},{6,2},{7,3},{8,4},{9,5},{1... | collective-permute-start | bytes 1769480 | tf_op jit(solution)/shard_map/ppermute | solution.py:344
  107.5 1.5 collective-permute-start.12
  109.0 18.3 %collective-permute-done.15.refs_0_ = bf16[2,2,12,16,384]{4,3,2,1,0:T(8,128)(2,1)S(1)} collective-permute-done((bf16[2,2,12,16,384]{4,3,2,1,0:T(8,128)(2,1)S(1)}, bf16[2,2,12,16,384]{4,3,2,1,0:T(8,128)(2,1)S(1)}, u32[]{:S(2)}, u32[]{:S(2)}) %collective-permute-start.15) | collective-permute-done | bytes 589856 | tf_op jit(solution)/shard_map/ppermute | solution.py:344
  127.3 2.6 %collective-permute-start.13 = (bf16[3,2,2,48,384]{4,3,2,1,0:T(8,128)(2,1)S(1)}, bf16[3,2,2,48,384]{4,3,2,1,0:T(8,128)(2,1)S(1)}, u32[]{:S(2)}, u32[]{:S(2)}) collective-permute-start(bf16[3,2,2,48,384]{4,3,2,1,0:T(8,128)(2,1)S(1)} %get-tuple-element.33), channel_id=1, source_target_pairs={{0,2},{1,3},{2,0},{3,1},{4,6},{5,7},{6,4},{7,5},{8,10},{9,11},{10,... | collective-permute-start | bytes 1327112 | tf_op jit(solution)/shard_map/ppermute | solution.py:347
  131.0 1.8 %place.2.refs_2_ = bf16[2,2,12,128,384]{4,3,2,1,0:T(8,128)(2,1)} custom-call(s32[4]{0:T(128)S(1)} %compare_select_fusion.2.pos_ref, bf16[384,384]{1,0:T(8,128)(2,1)S(1)} %get-tuple-element.23.refs_0_.hot_ref, bf16[192,192]{1,0:T(8,128)(2,1)S(1)} %get-tuple-element.21.rows_ref, bf16[5,2,2,48,384]{4,3,2,1,0:T(8,128)(2,1)S(1)} %get-tuple-element.24.refs_0_, ...), custom_call_target="tpu_custom_call" | custom-call | tf_op jit(solution)/shard_map/place/pallas_call | solution.py:298
  132.9 1.6 %deliver.2.refs_6_ = bf16[2,2,12,128,384]{4,3,2,1,0:T(8,128)(2,1)} custom-call(s32[4]{0:T(128)S(1)} %compare_select_fusion.2.pos_ref, bf16[2,2,12,16,384]{4,3,2,1,0:T(8,128)(2,1)S(1)} %collective-permute-done.15.refs_0_, bf16[2,2,12,16,384]{4,3,2,1,0:T(8,128)(2,1)S(1)} %collective-permute-done.16.refs_1_, ...), custom_call_target="tpu_custom_call", output_to_operand_aliasing={{}: (3, {})} | custom-call | tf_op jit(solution)/shard_map/deliver/pallas_call | solution.py:250
  134.5 5.5 %collective-permute-done.13.refs_4_ = bf16[3,2,2,48,384]{4,3,2,1,0:T(8,128)(2,1)S(1)} collective-permute-done((bf16[3,2,2,48,384]{4,3,2,1,0:T(8,128)(2,1)S(1)}, bf16[3,2,2,48,384]{4,3,2,1,0:T(8,128)(2,1)S(1)}, u32[]{:S(2)}, u32[]{:S(2)}) %collective-permute-start.13) | collective-permute-done | bytes 442400 | tf_op jit(solution)/shard_map/ppermute | solution.py:347
  140.0 10.2 %collective-permute-done.14.refs_5_ = bf16[3,2,2,48,384]{4,3,2,1,0:T(8,128)(2,1)S(1)} collective-permute-done((bf16[3,2,2,48,384]{4,3,2,1,0:T(8,128)(2,1)S(1)}, bf16[3,2,2,48,384]{4,3,2,1,0:T(8,128)(2,1)S(1)}, u32[]{:S(2)}, u32[]{:S(2)}) %collective-permute-start.14) | collective-permute-done | bytes 442400 | tf_op jit(solution)/shard_map/ppermute | solution.py:347
  150.2 4.9 %place.3.refs_2_ = bf16[2,2,12,128,384]{4,3,2,1,0:T(8,128)(2,1)} custom-call(s32[4]{0:T(128)S(1)} %compare_select_fusion.2.pos_ref, bf16[384,384]{1,0:T(8,128)(2,1)S(1)} %get-tuple-element.23.refs_0_.hot_ref, bf16[192,192]{1,0:T(8,128)(2,1)S(1)} %get-tuple-element.21.rows_ref, ...), custom_call_target="tpu_custom_call", output_to_operand_aliasing={{}: (9, {})} | custom-call | tf_op jit(solution)/shard_map/place/pallas_call | solution.py:298
  155.1 1.6 %deliver.3 = bf16[2,2,12,128,384]{4,3,2,1,0:T(8,128)(2,1)} custom-call(s32[4]{0:T(128)S(1)} %compare_select_fusion.2.pos_ref, bf16[2,2,12,16,384]{4,3,2,1,0:T(8,128)(2,1)S(1)} %collective-permute-done.7.refs_0_, bf16[2,2,12,16,384]{4,3,2,1,0:T(8,128)(2,1)S(1)} %collective-permute-done.8.refs_1_, ...), custom_call_target="tpu_custom_call", output_to_operand_aliasing={{}: (3, {})} | custom-call | tf_op jit(solution)/shard_map/deliver/pallas_call | solution.py:250
  (27 shorter events, 12.4 us)
Async XLA Ops:
  0.7 4.4 %collective-permute-start.1 = (f32[4,2,4,256]{3,2,1,0:T(4,128)S(1)}, f32[4,2,4,256]{3,2,1,0:T(4,128)S(1)}, u32[]{:S(2)}, u32[]{:S(2)}) collective-permute-start(f32[4,2,4,256]{3,2,1,0:T(4,128)S(1)} %get-tuple-element.38), channel_id=1, source_target_pairs={{0,128},{32,160},{64,192},{96,224},{128,0},{160,32},{192,64},{224,... | collective-permute-start | bytes 98312 | tf_op jit(solution)/shard_map/ppermute | solution.py:327
  2.0 3.1 %collective-permute-start = (f32[4,2,4,256]{3,2,1,0:T(4,128)S(1)}, f32[4,2,4,256]{3,2,1,0:T(4,128)S(1)}, u32[]{:S(2)}, u32[]{:S(2)}) collective-permute-start(f32[4,2,4,256]{3,2,1,0:T(4,128)S(1)} %get-tuple-element.38), channel_id=1, source_target_pairs={{0,64},{32,96},{64,128},{96,160},{128,192},{160,224},{192,0},{224,... | collective-permute-start | bytes 98312 | tf_op jit(solution)/shard_map/ppermute | solution.py:327
  3.8 4.0 %collective-permute-start.2 = (f32[4,2,4,256]{3,2,1,0:T(4,128)S(1)}, f32[4,2,4,256]{3,2,1,0:T(4,128)S(1)}, u32[]{:S(2)}, u32[]{:S(2)}) collective-permute-start(f32[4,2,4,256]{3,2,1,0:T(4,128)S(1)} %get-tuple-element.38), channel_id=1, source_target_pairs={{0,192},{32,224},{64,0},{96,32},{128,64},{160,96},{192,128},{224,1... | collective-permute-start | bytes 98312 | tf_op jit(solution)/shard_map/ppermute | solution.py:327
  7.8 6.3 %collective-permute-start.3 = (f32[4,4,2,4,256]{4,3,2,1,0:T(4,128)S(1)}, f32[4,4,2,4,256]{4,3,2,1,0:T(4,128)S(1)}, u32[]{:S(2)}, u32[]{:S(2)}) collective-permute-start(f32[4,4,2,4,256]{4,3,2,1,0:T(4,128)S(1)} %pad_maximum_fusion.mine_ref), channel_id=1, source_target_pairs={{0,32},{32,0},{64,96},{96,64},{128,160},{160,128},{192,224},{224,1... | collective-permute-start | bytes 393224 | tf_op jit(solution)/shard_map/ppermute | solution.py:334
  24.0 16.5 %collective-permute-start.4 = (bf16[5,2,2,48,384]{4,3,2,1,0:T(8,128)(2,1)S(1)}, bf16[5,2,2,48,384]{4,3,2,1,0:T(8,128)(2,1)S(1)}, u32[]{:S(2)}, u32[]{:S(2)}) collective-permute-start(bf16[5,2,2,48,384]{4,3,2,1,0:T(8,128)(2,1)S(1)} %get-tuple-element.25), channel_id=1, source_target_pairs={{0,1},{1,0},{2,3},{3,2},{4,5},{5,4},{6,7},{7,6},{8,9},{9,8},{10,11... | collective-permute-start | bytes 2211848 | tf_op jit(solution)/shard_map/ppermute | solution.py:347
  26.7 19.4 %collective-permute-start.5 = (bf16[5,2,2,48,384]{4,3,2,1,0:T(8,128)(2,1)S(1)}, bf16[5,2,2,48,384]{4,3,2,1,0:T(8,128)(2,1)S(1)}, u32[]{:S(2)}, u32[]{:S(2)}) collective-permute-start(bf16[5,2,2,48,384]{4,3,2,1,0:T(8,128)(2,1)S(1)} %get-tuple-element.26), channel_id=1, source_target_pairs={{0,2},{1,3},{2,0},{3,1},{4,6},{5,7},{6,4},{7,5},{8,10},{9,11},{10,... | collective-permute-start | bytes 2211848 | tf_op jit(solution)/shard_map/ppermute | solution.py:347
  29.4 33.2 %collective-permute-start.6 = (bf16[5,2,2,48,384]{4,3,2,1,0:T(8,128)(2,1)S(1)}, bf16[5,2,2,48,384]{4,3,2,1,0:T(8,128)(2,1)S(1)}, u32[]{:S(2)}, u32[]{:S(2)}) collective-permute-start(bf16[5,2,2,48,384]{4,3,2,1,0:T(8,128)(2,1)S(1)} %get-tuple-element.27), channel_id=1, source_target_pairs={{0,3},{1,2},{2,1},{3,0},{4,7},{5,6},{6,5},{7,4},{8,11},{9,10},{10,... | collective-permute-start | bytes 2211848 | tf_op jit(solution)/shard_map/ppermute | solution.py:347
  31.7 37.1 %collective-permute-start.9 = (bf16[4,2,2,48,384]{4,3,2,1,0:T(8,128)(2,1)S(1)}, bf16[4,2,2,48,384]{4,3,2,1,0:T(8,128)(2,1)S(1)}, u32[]{:S(2)}, u32[]{:S(2)}) collective-permute-start(bf16[4,2,2,48,384]{4,3,2,1,0:T(8,128)(2,1)S(1)} %flow.4), channel_id=1, source_target_pairs={{0,16},{1,17},{2,18},{3,19},{4,20},{5,21},{6,22},{7,23},{8,24},{9,... | collective-permute-start | bytes 1769480 | tf_op jit(solution)/shard_map/ppermute | solution.py:344
  40.4 60.9 %collective-permute-start.10 = (bf16[4,2,2,48,384]{4,3,2,1,0:T(8,128)(2,1)S(1)}, bf16[4,2,2,48,384]{4,3,2,1,0:T(8,128)(2,1)S(1)}, u32[]{:S(2)}, u32[]{:S(2)}) collective-permute-start(bf16[4,2,2,48,384]{4,3,2,1,0:T(8,128)(2,1)S(1)} %get-tuple-element.30), channel_id=1, source_target_pairs={{0,12},{1,13},{2,14},{3,15},{4,16},{5,17},{6,18},{7,19},{8,20},{9,... | collective-permute-start | bytes 1769480 | tf_op jit(solution)/shard_map/ppermute | solution.py:344
  40.5 66.9 %collective-permute-start.11 = (bf16[4,2,2,48,384]{4,3,2,1,0:T(8,128)(2,1)S(1)}, bf16[4,2,2,48,384]{4,3,2,1,0:T(8,128)(2,1)S(1)}, u32[]{:S(2)}, u32[]{:S(2)}) collective-permute-start(bf16[4,2,2,48,384]{4,3,2,1,0:T(8,128)(2,1)S(1)} %get-tuple-element.31), channel_id=1, source_target_pairs={{0,20},{1,21},{2,22},{3,23},{4,24},{5,25},{6,26},{7,27},{8,28},{9,... | collective-permute-start | bytes 1769480 | tf_op jit(solution)/shard_map/ppermute | solution.py:344
  63.5 63.8 %collective-permute-start.15 = (bf16[2,2,12,16,384]{4,3,2,1,0:T(8,128)(2,1)S(1)}, bf16[2,2,12,16,384]{4,3,2,1,0:T(8,128)(2,1)S(1)}, u32[]{:S(2)}, u32[]{:S(2)}) collective-permute-start(bf16[2,2,12,16,384]{4,3,2,1,0:T(8,128)(2,1)S(1)} %get-tuple-element.35), channel_id=1, source_target_pairs={{0,8},{1,9},{2,10},{3,11},{4,12},{5,13},{6,14},{7,15},{8,16},{9,17... | collective-permute-start | bytes 1769480 | tf_op jit(solution)/shard_map/ppermute | solution.py:344
  66.6 63.3 %collective-permute-start.16 = (bf16[2,2,12,16,384]{4,3,2,1,0:T(8,128)(2,1)S(1)}, bf16[2,2,12,16,384]{4,3,2,1,0:T(8,128)(2,1)S(1)}, u32[]{:S(2)}, u32[]{:S(2)}) collective-permute-start(bf16[2,2,12,16,384]{4,3,2,1,0:T(8,128)(2,1)S(1)} %get-tuple-element.36), channel_id=1, source_target_pairs={{0,24},{1,25},{2,26},{3,27},{4,28},{5,29},{6,30},{7,31},{8,0},{9,1... | collective-permute-start | bytes 1769480 | tf_op jit(solution)/shard_map/ppermute | solution.py:344
  68.8 86.2 %collective-permute-start.7 = (bf16[2,2,12,16,384]{4,3,2,1,0:T(8,128)(2,1)S(1)}, bf16[2,2,12,16,384]{4,3,2,1,0:T(8,128)(2,1)S(1)}, u32[]{:S(2)}, u32[]{:S(2)}) collective-permute-start(bf16[2,2,12,16,384]{4,3,2,1,0:T(8,128)(2,1)S(1)} %get-tuple-element.28), channel_id=1, source_target_pairs={{0,4},{1,5},{2,6},{3,7},{4,8},{5,9},{6,10},{7,11},{8,12},{9,13},{1... | collective-permute-start | bytes 1769480 | tf_op jit(solution)/shard_map/ppermute | solution.py:344
  101.4 53.7 %collective-permute-start.8 = (bf16[2,2,12,16,384]{4,3,2,1,0:T(8,128)(2,1)S(1)}, bf16[2,2,12,16,384]{4,3,2,1,0:T(8,128)(2,1)S(1)}, u32[]{:S(2)}, u32[]{:S(2)}) collective-permute-start(bf16[2,2,12,16,384]{4,3,2,1,0:T(8,128)(2,1)S(1)} %get-tuple-element.29), channel_id=1, source_target_pairs={{0,28},{1,29},{2,30},{3,31},{4,0},{5,1},{6,2},{7,3},{8,4},{9,5},{1... | collective-permute-start | bytes 1769480 | tf_op jit(solution)/shard_map/ppermute | solution.py:344
  107.5 26.9 %collective-permute-start.12 = (bf16[3,2,2,48,384]{4,3,2,1,0:T(8,128)(2,1)S(1)}, bf16[3,2,2,48,384]{4,3,2,1,0:T(8,128)(2,1)S(1)}, u32[]{:S(2)}, u32[]{:S(2)}) collective-permute-start(bf16[3,2,2,48,384]{4,3,2,1,0:T(8,128)(2,1)S(1)} %get-tuple-element.32), channel_id=1, source_target_pairs={{0,1},{1,0},{2,3},{3,2},{4,5},{5,4},{6,7},{7,6},{8,9},{9,8},{10,11... | collective-permute-start | bytes 1327112 | tf_op jit(solution)/shard_map/ppermute | solution.py:347
  127.3 12.7 %collective-permute-start.13 = (bf16[3,2,2,48,384]{4,3,2,1,0:T(8,128)(2,1)S(1)}, bf16[3,2,2,48,384]{4,3,2,1,0:T(8,128)(2,1)S(1)}, u32[]{:S(2)}, u32[]{:S(2)}) collective-permute-start(bf16[3,2,2,48,384]{4,3,2,1,0:T(8,128)(2,1)S(1)} %get-tuple-element.33), channel_id=1, source_target_pairs={{0,2},{1,3},{2,0},{3,1},{4,6},{5,7},{6,4},{7,5},{8,10},{9,11},{10,... | collective-permute-start | bytes 1327112 | tf_op jit(solution)/shard_map/ppermute | solution.py:347
  129.9 20.3 %collective-permute-start.14 = (bf16[3,2,2,48,384]{4,3,2,1,0:T(8,128)(2,1)S(1)}, bf16[3,2,2,48,384]{4,3,2,1,0:T(8,128)(2,1)S(1)}, u32[]{:S(2)}, u32[]{:S(2)}) collective-permute-start(bf16[3,2,2,48,384]{4,3,2,1,0:T(8,128)(2,1)S(1)} %get-tuple-element.34), channel_id=1, source_target_pairs={{0,3},{1,2},{2,1},{3,0},{4,7},{5,6},{6,5},{7,4},{8,11},{9,10},{10,... | collective-permute-start | bytes 1327112 | tf_op jit(solution)/shard_map/ppermute | solution.py:347

commit v4 on v3

--- a/solution.py
+++ b/solution.py
@@ -95,22 +95,6 @@
     out_ref[...] = out + jnp.dot(high, hot, preferred_element_type=jnp.float32)
 
 
-def bubble_of(pos, mine, other, sites):
-    loop = 2 * 2 * mine.shape[0] * mine.shape[2] // 2
-    return pl.pallas_call(
-        bubble_kernel,
-        in_specs=[SMEM, VMEM, VMEM, VMEM],
-        out_specs=VMEM,
-        out_shape=jax.ShapeDtypeStruct((16, sites.shape[1]), jnp.float32),
-        scratch_shapes=[
-            pltpu.VMEM((4, loop) + mine.shape[3:], jnp.float32),
-            pltpu.VMEM((16, mine.shape[-1]), jnp.float32),
-        ],
-        compiler_params=params(),
-        name="bubble",
-    )(pos, mine, other, sites)
-
-
 def flow_kernel(dzs, by_plane, unroll, pos_ref, mask_ref, gamma_ref, bubble_ref, *refs):
     hot_ref, *outs, scratch = refs if unroll is False else (None, *refs)
     planes = len(dzs)
@@ -189,6 +173,34 @@
     )(pos, mask, gamma, bubble, *hot)
 
 
+def first_kernel(dzs, pos_ref, mask_ref, gamma_ref, mine_ref, other_ref, site_ref, *refs):
+    *outs, bubble_ref, all_ref, sum_ref, scratch = refs
+    bubble_kernel(pos_ref, mine_ref, other_ref, site_ref, bubble_ref, all_ref, sum_ref)
+    flow_kernel(dzs, True, True, pos_ref, mask_ref, gamma_ref, bubble_ref, *outs, scratch)
+
+
+def first_flows(pos, mask, gamma, mine, other, sites, dzs):
+    _, count, order, _ = gamma.shape
+    planes = len(dzs)
+    height = order // 8
+    loop = 2 * mine.shape[0] * mine.shape[2]
+    *bundles, bubble = pl.pallas_call(
+        functools.partial(first_kernel, dzs),
+        in_specs=[SMEM, SMEM] + [VMEM] * 4,
+        out_specs=[VMEM] * (planes + 1),
+        scratch_shapes=[
+            pltpu.VMEM((4, loop) + mine.shape[3:], jnp.float32),
+            pltpu.VMEM((16, mine.shape[-1]), jnp.float32),
+            pltpu.VMEM((2, planes, PLANE, count // 2, height // PLANE, order), jnp.float32),
+        ],
+        out_shape=[jax.ShapeDtypeStruct((PLANE, 2, 2, height, order), jnp.bfloat16)] * planes
+        + [jax.ShapeDtypeStruct((16, order), jnp.float32)],
+        compiler_params=params(),
+        name="first_flow",
+    )(pos, mask, gamma, mine, other, sites)
+    return bundles, bubble
+
+
 def turn(arrays, outer):
     _, *rest = arrays[0].shape
     shape = jax.ShapeDtypeStruct((len(arrays), *rest), arrays[0].dtype)
@@ -337,7 +349,6 @@
     perm = site_perm.reshape(1, order)
     sites = bond_site.reshape(1, order)
     gamma, *ones = tables(pos, perm, gamma)
-    bubble = bubble_of(pos, mine, other, sites)
 
     def along_z(a, dz):
         hops = [(i * PLANE + p, ((i + dz) % deep) * PLANE + p) for i in range(deep) for p in range(PLANE)]
@@ -346,11 +357,11 @@
     def in_plane(a, d):
         return lax.ppermute(a, "bond", [(i, i ^ d) for i in range(bonds)])
 
+    bundles, bubble = first_flows(pos, causal_mask, gamma, mine, other, sites, HALF)
+    early = [along_z(a, dz) for a, dz in zip(bundles, HALF)]
     flow = functools.partial(flows, pos, causal_mask, gamma, bubble)
-    early = []
-    for dzs in (HALF, FAR):
-        bundles = flow(dzs, True)
-        early += [along_z(a, dz) for a, dz in zip(bundles, dzs)]
+    bundles = flow(FAR, True)
+    early += [along_z(a, dz) for a, dz in zip(bundles, FAR)]
     sets = flow(LATE, False, ones[0])
     sets = [sets[0]] + [in_plane(sets[d], d) for d in range(1, PLANE)]
     bundles = order_rows(ones[1], sets)

time: 157 us -> 157 us (level)
    ppermute x6, waiting for transfers between devices: 33.3 us -> 35.2 us  [in_plane(): return lax.ppermute(a, 'bond', [(i, i ^ d) for i in range(bonds)])]
    ppermute x7, waiting for transfers between devices: 50.2 us -> 48.4 us  [along_z(): return lax.ppermute(a, 'bond', hops)]
    pallas_call x3 -> x2, Pallas kernels: 13.3 us -> 11.6 us  [flows(): pl.pallas_call(functools.partial(flow_kernel, dzs, by_plane, not hot), in...]
  transfers between devices with their start and end apart: 17 -> 17, of which waited for: 8 -> 8; matrix products, arithmetic and copies ran while one was open for 1% -> 1% of each run, Pallas kernels for 11% -> 9%
where the time goes in v4:
time: 157 us; the launch traced here: 156 us
  waiting for transfers between devices  87.6 us (56%)
  starting transfers between devices  38 us (24%)
  Pallas kernels  27.5 us (18%)
  local copies, waits for them, and re-layouts  2.05 us (1%)
    ppermute x7, waiting for transfers between devices, along_z(): return lax.ppermute(a, 'bond', hops)  48.4 us
    ppermute x6, waiting for transfers between devices, in_plane(): return lax.ppermute(a, 'bond', [(i, i ^ d) for i in range(bonds)])  35.2 us
    ppermute x7, starting transfers between devices, along_z(): return lax.ppermute(a, 'bond', hops)  22.5 us
    pallas_call x2, Pallas kernels, flows(): pl.pallas_call(functools.partial(flow_kernel, dzs, by_plane, not hot), in...  11.6 us
    ppermute x6, starting transfers between devices, in_plane(): return lax.ppermute(a, 'bond', [(i, i ^ d) for i in range(bonds)])  11.1 us
    pallas_call x2, Pallas kernels, place(): pl.pallas_call(functools.partial(place_kernel, units, dzs[0] not in LATE)...  6.68 us
    ppermute x3, waiting for transfers between devices, along_x(): lax.ppermute(a, 'freq', [(2 * x + y, 2 * ((x + d) % 4) + y) for x in rang...  3.97 us
    pallas_call x2, Pallas kernels, deliver(): pl.pallas_call(functools.partial(deliver_kernel, dzs), in_specs=[SMEM] +...  3.17 us
  transfers between devices with their start and end apart: 17, of which 8 were waited for; matrix products, arithmetic and copies ran while one was open for 1% of the time, Pallas kernels for 9%

profile of v4, /device:TPU:39, one launch (start us, length us, event | category | flops | bytes accessed | tf_op | source)
XLA Modules:
  0.0 156.2 jit_solution(6914603027987168588)
XLA Ops:
  2.0 1.8 %collective-permute-start = (f32[4,2,4,256]{3,2,1,0:T(4,128)S(1)}, f32[4,2,4,256]{3,2,1,0:T(4,128)S(1)}, u32[]{:S(2)}, u32[]{:S(2)}) collective-permute-start(f32[4,2,4,256]{3,2,1,0:T(4,128)S(1)} %get-tuple-element.42), channel_id=1, source_target_pairs={{0,64},{32,96},{64,128},{96,160},{128,192},{160,224},{192,0},{224,... | collective-permute-start | bytes 98312 | tf_op jit(solution)/shard_map/ppermute | solution.py:339
  5.1 2.6 %collective-permute-done.2 = f32[4,2,4,256]{3,2,1,0:T(4,128)S(1)} collective-permute-done((f32[4,2,4,256]{3,2,1,0:T(4,128)S(1)}, f32[4,2,4,256]{3,2,1,0:T(4,128)S(1)}, u32[]{:S(2)}, u32[]{:S(2)}) %collective-permute-start.2) | collective-permute-done | bytes 32800 | tf_op jit(solution)/shard_map/ppermute | solution.py:339
  11.2 2.9 %tables.1 = (bf16[2,8,384,384]{3,2,1,0:T(8,128)(2,1)S(1)}, bf16[384,384]{1,0:T(8,128)(2,1)S(1)}, bf16[192,192]{1,0:T(8,128)(2,1)S(1)}) custom-call(s32[4]{0:T(128)S(1)} %compare_select_fusion.2.pos_ref, s32[1,384]{1,0:T(1,128)S(1)} %reshape.9.perm_ref, bf16[2,8,384,384]{3,2,1,0:T(8,128)(2,1)} %bitcast.6), custom_call_target="tpu_custom_call" | custom-call | tf_op jit(solution)/shard_map/tables/pallas_call | solution.py:48
  14.1 2.1 %first_flow.1 = (bf16[4,2,2,48,384]{4,3,2,1,0:T(8,128)(2,1)S(1)}, f32[16,384]{1,0:T(8,128)S(1)}) custom-call(s32[4]{0:T(128)S(1)} %compare_select_fusion.2.pos_ref, s32[2,3,3]{2,1,0:T(4,128)S(1)} %copy.11.mask_ref, bf16[2,8,384,384]{3,2,1,0:T(8,128)(2,1)S(1)} %get-tuple-element.24.gamma_ref, f32[4,4,2,4,256]{4,3,2,1,0:T(4,128)S(1)} %pad_maximum_fusion.mine_ref, ...), custom_call_target="tpu_custom_call" | custom-call | tf_op jit(solution)/shard_map/first_flow/pallas_call | solution.py:187
  16.3 9.0 %flow.2 = (bf16[5,2,2,48,384]{4,3,2,1,0:T(8,128)(2,1)S(1)}, bf16[5,2,2,48,384]{4,3,2,1,0:T(8,128)(2,1)S(1)}, bf16[5,2,2,48,384]{4,3,2,1,0:T(8,128)(2,1)S(1)}, bf16[5,2,2,48,384]{4,3,2,1,0:T(8,128)(2,1)S(1)}) custom-call(s32[4]{0:T(128)S(1)} %compare_select_fusion.2.pos_ref, s32[2,3,3]{2,1,0:T(4,128)S(1)} %copy.11.mask_ref, ...), custom_call_target="tpu_custom_call" | custom-call | tf_op jit(solution)/shard_map/flow/pallas_call | solution.py:165
  25.3 2.8 %collective-permute-start.4 = (bf16[5,2,2,48,384]{4,3,2,1,0:T(8,128)(2,1)S(1)}, bf16[5,2,2,48,384]{4,3,2,1,0:T(8,128)(2,1)S(1)}, u32[]{:S(2)}, u32[]{:S(2)}) collective-permute-start(bf16[5,2,2,48,384]{4,3,2,1,0:T(8,128)(2,1)S(1)} %get-tuple-element.28), channel_id=1, source_target_pairs={{0,1},{1,0},{2,3},{3,2},{4,5},{5,4},{6,7},{7,6},{8,9},{9,8},{10,11... | collective-permute-start | bytes 2211848 | tf_op jit(solution)/shard_map/ppermute | solution.py:358
  28.1 2.6 %collective-permute-start.5 = (bf16[5,2,2,48,384]{4,3,2,1,0:T(8,128)(2,1)S(1)}, bf16[5,2,2,48,384]{4,3,2,1,0:T(8,128)(2,1)S(1)}, u32[]{:S(2)}, u32[]{:S(2)}) collective-permute-start(bf16[5,2,2,48,384]{4,3,2,1,0:T(8,128)(2,1)S(1)} %get-tuple-element.29), channel_id=1, source_target_pairs={{0,2},{1,3},{2,0},{3,1},{4,6},{5,7},{6,4},{7,5},{8,10},{9,11},{10,... | collective-permute-start | bytes 2211848 | tf_op jit(solution)/shard_map/ppermute | solution.py:358
  31.3 6.0 %collective-permute-start.9 = (bf16[4,2,2,48,384]{4,3,2,1,0:T(8,128)(2,1)S(1)}, bf16[4,2,2,48,384]{4,3,2,1,0:T(8,128)(2,1)S(1)}, u32[]{:S(2)}, u32[]{:S(2)}) collective-permute-start(bf16[4,2,2,48,384]{4,3,2,1,0:T(8,128)(2,1)S(1)} %get-tuple-element.33), channel_id=1, source_target_pairs={{0,16},{1,17},{2,18},{3,19},{4,20},{5,21},{6,22},{7,23},{8,24},{9,... | collective-permute-start | bytes 1769480 | tf_op jit(solution)/shard_map/ppermute | solution.py:355
  37.3 2.5 %flow.3 = (bf16[4,2,2,48,384]{4,3,2,1,0:T(8,128)(2,1)S(1)}, bf16[4,2,2,48,384]{4,3,2,1,0:T(8,128)(2,1)S(1)}) custom-call(s32[4]{0:T(128)S(1)} %compare_select_fusion.2.pos_ref, s32[2,3,3]{2,1,0:T(4,128)S(1)} %copy.11.mask_ref, bf16[2,8,384,384]{3,2,1,0:T(8,128)(2,1)S(1)} %get-tuple-element.24.gamma_ref, f32[16,384]{1,0:T(8,128)S(1)} %get-tuple-element.25.bubble_ref), custom_call_target="tpu_custom_call" | custom-call | tf_op jit(solution)/shard_map/flow/pallas_call | solution.py:165
  40.0 4.5 %collective-permute-start.11 = (bf16[4,2,2,48,384]{4,3,2,1,0:T(8,128)(2,1)S(1)}, bf16[4,2,2,48,384]{4,3,2,1,0:T(8,128)(2,1)S(1)}, u32[]{:S(2)}, u32[]{:S(2)}) collective-permute-start(bf16[4,2,2,48,384]{4,3,2,1,0:T(8,128)(2,1)S(1)} %get-tuple-element.35), channel_id=1, source_target_pairs={{0,20},{1,21},{2,22},{3,23},{4,24},{5,25},{6,26},{7,27},{8,28},{9,... | collective-permute-start | bytes 1769480 | tf_op jit(solution)/shard_map/ppermute | solution.py:355
  44.4 3.1 %collective-permute-done.5.refs_2_ = bf16[5,2,2,48,384]{4,3,2,1,0:T(8,128)(2,1)S(1)} collective-permute-done((bf16[5,2,2,48,384]{4,3,2,1,0:T(8,128)(2,1)S(1)}, bf16[5,2,2,48,384]{4,3,2,1,0:T(8,128)(2,1)S(1)}, u32[]{:S(2)}, u32[]{:S(2)}) %collective-permute-start.5) | collective-permute-done | bytes 737312 | tf_op jit(solution)/shard_map/ppermute | solution.py:358
  47.5 16.4 %collective-permute-done.6.refs_3_ = bf16[5,2,2,48,384]{4,3,2,1,0:T(8,128)(2,1)S(1)} collective-permute-done((bf16[5,2,2,48,384]{4,3,2,1,0:T(8,128)(2,1)S(1)}, bf16[5,2,2,48,384]{4,3,2,1,0:T(8,128)(2,1)S(1)}, u32[]{:S(2)}, u32[]{:S(2)}) %collective-permute-start.6) | collective-permute-done | bytes 737312 | tf_op jit(solution)/shard_map/ppermute | solution.py:358
  64.9 3.1 %collective-permute-start.15 = (bf16[2,2,12,16,384]{4,3,2,1,0:T(8,128)(2,1)S(1)}, bf16[2,2,12,16,384]{4,3,2,1,0:T(8,128)(2,1)S(1)}, u32[]{:S(2)}, u32[]{:S(2)}) collective-permute-start(bf16[2,2,12,16,384]{4,3,2,1,0:T(8,128)(2,1)S(1)} %get-tuple-element.39), channel_id=1, source_target_pairs={{0,8},{1,9},{2,10},{3,11},{4,12},{5,13},{6,14},{7,15},{8,16},{9,17... | collective-permute-start | bytes 1769480 | tf_op jit(solution)/shard_map/ppermute | solution.py:355
  67.9 2.2 %collective-permute-start.16 = (bf16[2,2,12,16,384]{4,3,2,1,0:T(8,128)(2,1)S(1)}, bf16[2,2,12,16,384]{4,3,2,1,0:T(8,128)(2,1)S(1)}, u32[]{:S(2)}, u32[]{:S(2)}) collective-permute-start(bf16[2,2,12,16,384]{4,3,2,1,0:T(8,128)(2,1)S(1)} %get-tuple-element.40), channel_id=1, source_target_pairs={{0,24},{1,25},{2,26},{3,27},{4,28},{5,29},{6,30},{7,31},{8,0},{9,1... | collective-permute-start | bytes 1769480 | tf_op jit(solution)/shard_map/ppermute | solution.py:355
  70.8 30.1 %collective-permute-done.10.refs_1_ = bf16[4,2,2,48,384]{4,3,2,1,0:T(8,128)(2,1)S(1)} collective-permute-done((bf16[4,2,2,48,384]{4,3,2,1,0:T(8,128)(2,1)S(1)}, bf16[4,2,2,48,384]{4,3,2,1,0:T(8,128)(2,1)S(1)}, u32[]{:S(2)}, u32[]{:S(2)}) %collective-permute-start.10) | collective-permute-done | bytes 589856 | tf_op jit(solution)/shard_map/ppermute | solution.py:355
  100.8 6.0 %collective-permute-start.8 = (bf16[2,2,12,16,384]{4,3,2,1,0:T(8,128)(2,1)S(1)}, bf16[2,2,12,16,384]{4,3,2,1,0:T(8,128)(2,1)S(1)}, u32[]{:S(2)}, u32[]{:S(2)}) collective-permute-start(bf16[2,2,12,16,384]{4,3,2,1,0:T(8,128)(2,1)S(1)} %get-tuple-element.32), channel_id=1, source_target_pairs={{0,28},{1,29},{2,30},{3,31},{4,0},{5,1},{6,2},{7,3},{8,4},{9,5},{1... | collective-permute-start | bytes 1769480 | tf_op jit(solution)/shard_map/ppermute | solution.py:355
  108.4 18.3 %collective-permute-done.15.refs_0_ = bf16[2,2,12,16,384]{4,3,2,1,0:T(8,128)(2,1)S(1)} collective-permute-done((bf16[2,2,12,16,384]{4,3,2,1,0:T(8,128)(2,1)S(1)}, bf16[2,2,12,16,384]{4,3,2,1,0:T(8,128)(2,1)S(1)}, u32[]{:S(2)}, u32[]{:S(2)}) %collective-permute-start.15) | collective-permute-done | bytes 589856 | tf_op jit(solution)/shard_map/ppermute | solution.py:355
  126.7 2.7 %collective-permute-start.13 = (bf16[3,2,2,48,384]{4,3,2,1,0:T(8,128)(2,1)S(1)}, bf16[3,2,2,48,384]{4,3,2,1,0:T(8,128)(2,1)S(1)}, u32[]{:S(2)}, u32[]{:S(2)}) collective-permute-start(bf16[3,2,2,48,384]{4,3,2,1,0:T(8,128)(2,1)S(1)} %get-tuple-element.37), channel_id=1, source_target_pairs={{0,2},{1,3},{2,0},{3,1},{4,6},{5,7},{6,4},{7,5},{8,10},{9,11},{10,... | collective-permute-start | bytes 1327112 | tf_op jit(solution)/shard_map/ppermute | solution.py:358
  130.4 1.8 %place.2.refs_2_ = bf16[2,2,12,128,384]{4,3,2,1,0:T(8,128)(2,1)} custom-call(s32[4]{0:T(128)S(1)} %compare_select_fusion.2.pos_ref, bf16[384,384]{1,0:T(8,128)(2,1)S(1)} %get-tuple-element.26.refs_0_.hot_ref, bf16[192,192]{1,0:T(8,128)(2,1)S(1)} %get-tuple-element.23.rows_ref, bf16[5,2,2,48,384]{4,3,2,1,0:T(8,128)(2,1)S(1)} %get-tuple-element.27.refs_0_, ...), custom_call_target="tpu_custom_call" | custom-call | tf_op jit(solution)/shard_map/place/pallas_call | solution.py:310
  132.3 1.6 %deliver.2.refs_6_ = bf16[2,2,12,128,384]{4,3,2,1,0:T(8,128)(2,1)} custom-call(s32[4]{0:T(128)S(1)} %compare_select_fusion.2.pos_ref, bf16[2,2,12,16,384]{4,3,2,1,0:T(8,128)(2,1)S(1)} %collective-permute-done.15.refs_0_, bf16[2,2,12,16,384]{4,3,2,1,0:T(8,128)(2,1)S(1)} %collective-permute-done.16.refs_1_, ...), custom_call_target="tpu_custom_call", output_to_operand_aliasing={{}: (3, {})} | custom-call | tf_op jit(solution)/shard_map/deliver/pallas_call | solution.py:262
  133.9 5.5 %collective-permute-done.13.refs_4_ = bf16[3,2,2,48,384]{4,3,2,1,0:T(8,128)(2,1)S(1)} collective-permute-done((bf16[3,2,2,48,384]{4,3,2,1,0:T(8,128)(2,1)S(1)}, bf16[3,2,2,48,384]{4,3,2,1,0:T(8,128)(2,1)S(1)}, u32[]{:S(2)}, u32[]{:S(2)}) %collective-permute-start.13) | collective-permute-done | bytes 442400 | tf_op jit(solution)/shard_map/ppermute | solution.py:358
  139.4 10.2 %collective-permute-done.14.refs_5_ = bf16[3,2,2,48,384]{4,3,2,1,0:T(8,128)(2,1)S(1)} collective-permute-done((bf16[3,2,2,48,384]{4,3,2,1,0:T(8,128)(2,1)S(1)}, bf16[3,2,2,48,384]{4,3,2,1,0:T(8,128)(2,1)S(1)}, u32[]{:S(2)}, u32[]{:S(2)}) %collective-permute-start.14) | collective-permute-done | bytes 442400 | tf_op jit(solution)/shard_map/ppermute | solution.py:358
  149.6 4.8 %place.3.refs_2_ = bf16[2,2,12,128,384]{4,3,2,1,0:T(8,128)(2,1)} custom-call(s32[4]{0:T(128)S(1)} %compare_select_fusion.2.pos_ref, bf16[384,384]{1,0:T(8,128)(2,1)S(1)} %get-tuple-element.26.refs_0_.hot_ref, bf16[192,192]{1,0:T(8,128)(2,1)S(1)} %get-tuple-element.23.rows_ref, ...), custom_call_target="tpu_custom_call", output_to_operand_aliasing={{}: (9, {})} | custom-call | tf_op jit(solution)/shard_map/place/pallas_call | solution.py:310
  154.5 1.6 %deliver.3 = bf16[2,2,12,128,384]{4,3,2,1,0:T(8,128)(2,1)} custom-call(s32[4]{0:T(128)S(1)} %compare_select_fusion.2.pos_ref, bf16[2,2,12,16,384]{4,3,2,1,0:T(8,128)(2,1)S(1)} %collective-permute-done.7.refs_0_, bf16[2,2,12,16,384]{4,3,2,1,0:T(8,128)(2,1)S(1)} %collective-permute-done.8.refs_1_, ...), custom_call_target="tpu_custom_call", output_to_operand_aliasing={{}: (3, {})} | custom-call | tf_op jit(solution)/shard_map/deliver/pallas_call | solution.py:262
  (26 shorter events, 11.6 us)
Async XLA Ops:
  0.7 4.4 %collective-permute-start.1 = (f32[4,2,4,256]{3,2,1,0:T(4,128)S(1)}, f32[4,2,4,256]{3,2,1,0:T(4,128)S(1)}, u32[]{:S(2)}, u32[]{:S(2)}) collective-permute-start(f32[4,2,4,256]{3,2,1,0:T(4,128)S(1)} %get-tuple-element.42), channel_id=1, source_target_pairs={{0,128},{32,160},{64,192},{96,224},{128,0},{160,32},{192,64},{224,... | collective-permute-start | bytes 98312 | tf_op jit(solution)/shard_map/ppermute | solution.py:339
  2.0 3.1 %collective-permute-start = (f32[4,2,4,256]{3,2,1,0:T(4,128)S(1)}, f32[4,2,4,256]{3,2,1,0:T(4,128)S(1)}, u32[]{:S(2)}, u32[]{:S(2)}) collective-permute-start(f32[4,2,4,256]{3,2,1,0:T(4,128)S(1)} %get-tuple-element.42), channel_id=1, source_target_pairs={{0,64},{32,96},{64,128},{96,160},{128,192},{160,224},{192,0},{224,... | collective-permute-start | bytes 98312 | tf_op jit(solution)/shard_map/ppermute | solution.py:339
  3.8 4.0 %collective-permute-start.2 = (f32[4,2,4,256]{3,2,1,0:T(4,128)S(1)}, f32[4,2,4,256]{3,2,1,0:T(4,128)S(1)}, u32[]{:S(2)}, u32[]{:S(2)}) collective-permute-start(f32[4,2,4,256]{3,2,1,0:T(4,128)S(1)} %get-tuple-element.42), channel_id=1, source_target_pairs={{0,192},{32,224},{64,0},{96,32},{128,64},{160,96},{192,128},{224,1... | collective-permute-start | bytes 98312 | tf_op jit(solution)/shard_map/ppermute | solution.py:339
  7.8 6.3 %collective-permute-start.3 = (f32[4,4,2,4,256]{4,3,2,1,0:T(4,128)S(1)}, f32[4,4,2,4,256]{4,3,2,1,0:T(4,128)S(1)}, u32[]{:S(2)}, u32[]{:S(2)}) collective-permute-start(f32[4,4,2,4,256]{4,3,2,1,0:T(4,128)S(1)} %pad_maximum_fusion.mine_ref), channel_id=1, source_target_pairs={{0,32},{32,0},{64,96},{96,64},{128,160},{160,128},{192,224},{224,1... | collective-permute-start | bytes 393224 | tf_op jit(solution)/shard_map/ppermute | solution.py:346
  25.3 14.6 %collective-permute-start.4 = (bf16[5,2,2,48,384]{4,3,2,1,0:T(8,128)(2,1)S(1)}, bf16[5,2,2,48,384]{4,3,2,1,0:T(8,128)(2,1)S(1)}, u32[]{:S(2)}, u32[]{:S(2)}) collective-permute-start(bf16[5,2,2,48,384]{4,3,2,1,0:T(8,128)(2,1)S(1)} %get-tuple-element.28), channel_id=1, source_target_pairs={{0,1},{1,0},{2,3},{3,2},{4,5},{5,4},{6,7},{7,6},{8,9},{9,8},{10,11... | collective-permute-start | bytes 2211848 | tf_op jit(solution)/shard_map/ppermute | solution.py:358
  28.1 19.4 %collective-permute-start.5 = (bf16[5,2,2,48,384]{4,3,2,1,0:T(8,128)(2,1)S(1)}, bf16[5,2,2,48,384]{4,3,2,1,0:T(8,128)(2,1)S(1)}, u32[]{:S(2)}, u32[]{:S(2)}) collective-permute-start(bf16[5,2,2,48,384]{4,3,2,1,0:T(8,128)(2,1)S(1)} %get-tuple-element.29), channel_id=1, source_target_pairs={{0,2},{1,3},{2,0},{3,1},{4,6},{5,7},{6,4},{7,5},{8,10},{9,11},{10,... | collective-permute-start | bytes 2211848 | tf_op jit(solution)/shard_map/ppermute | solution.py:358
  30.7 33.2 %collective-permute-start.6 = (bf16[5,2,2,48,384]{4,3,2,1,0:T(8,128)(2,1)S(1)}, bf16[5,2,2,48,384]{4,3,2,1,0:T(8,128)(2,1)S(1)}, u32[]{:S(2)}, u32[]{:S(2)}) collective-permute-start(bf16[5,2,2,48,384]{4,3,2,1,0:T(8,128)(2,1)S(1)} %get-tuple-element.30), channel_id=1, source_target_pairs={{0,3},{1,2},{2,1},{3,0},{4,7},{5,6},{6,5},{7,4},{8,11},{9,10},{10,... | collective-permute-start | bytes 2211848 | tf_op jit(solution)/shard_map/ppermute | solution.py:358
  31.3 38.8 %collective-permute-start.9 = (bf16[4,2,2,48,384]{4,3,2,1,0:T(8,128)(2,1)S(1)}, bf16[4,2,2,48,384]{4,3,2,1,0:T(8,128)(2,1)S(1)}, u32[]{:S(2)}, u32[]{:S(2)}) collective-permute-start(bf16[4,2,2,48,384]{4,3,2,1,0:T(8,128)(2,1)S(1)} %get-tuple-element.33), channel_id=1, source_target_pairs={{0,16},{1,17},{2,18},{3,19},{4,20},{5,21},{6,22},{7,23},{8,24},{9,... | collective-permute-start | bytes 1769480 | tf_op jit(solution)/shard_map/ppermute | solution.py:355
  39.9 61.0 %collective-permute-start.10 = (bf16[4,2,2,48,384]{4,3,2,1,0:T(8,128)(2,1)S(1)}, bf16[4,2,2,48,384]{4,3,2,1,0:T(8,128)(2,1)S(1)}, u32[]{:S(2)}, u32[]{:S(2)}) collective-permute-start(bf16[4,2,2,48,384]{4,3,2,1,0:T(8,128)(2,1)S(1)} %get-tuple-element.34), channel_id=1, source_target_pairs={{0,12},{1,13},{2,14},{3,15},{4,16},{5,17},{6,18},{7,19},{8,20},{9,... | collective-permute-start | bytes 1769480 | tf_op jit(solution)/shard_map/ppermute | solution.py:355
  40.0 66.9 %collective-permute-start.11 = (bf16[4,2,2,48,384]{4,3,2,1,0:T(8,128)(2,1)S(1)}, bf16[4,2,2,48,384]{4,3,2,1,0:T(8,128)(2,1)S(1)}, u32[]{:S(2)}, u32[]{:S(2)}) collective-permute-start(bf16[4,2,2,48,384]{4,3,2,1,0:T(8,128)(2,1)S(1)} %get-tuple-element.35), channel_id=1, source_target_pairs={{0,20},{1,21},{2,22},{3,23},{4,24},{5,25},{6,26},{7,27},{8,28},{9,... | collective-permute-start | bytes 1769480 | tf_op jit(solution)/shard_map/ppermute | solution.py:355
  64.9 61.9 %collective-permute-start.15 = (bf16[2,2,12,16,384]{4,3,2,1,0:T(8,128)(2,1)S(1)}, bf16[2,2,12,16,384]{4,3,2,1,0:T(8,128)(2,1)S(1)}, u32[]{:S(2)}, u32[]{:S(2)}) collective-permute-start(bf16[2,2,12,16,384]{4,3,2,1,0:T(8,128)(2,1)S(1)} %get-tuple-element.39), channel_id=1, source_target_pairs={{0,8},{1,9},{2,10},{3,11},{4,12},{5,13},{6,14},{7,15},{8,16},{9,17... | collective-permute-start | bytes 1769480 | tf_op jit(solution)/shard_map/ppermute | solution.py:355
  67.9 61.5 %collective-permute-start.16 = (bf16[2,2,12,16,384]{4,3,2,1,0:T(8,128)(2,1)S(1)}, bf16[2,2,12,16,384]{4,3,2,1,0:T(8,128)(2,1)S(1)}, u32[]{:S(2)}, u32[]{:S(2)}) collective-permute-start(bf16[2,2,12,16,384]{4,3,2,1,0:T(8,128)(2,1)S(1)} %get-tuple-element.40), channel_id=1, source_target_pairs={{0,24},{1,25},{2,26},{3,27},{4,28},{5,29},{6,30},{7,31},{8,0},{9,1... | collective-permute-start | bytes 1769480 | tf_op jit(solution)/shard_map/ppermute | solution.py:355
  70.1 84.3 %collective-permute-start.7 = (bf16[2,2,12,16,384]{4,3,2,1,0:T(8,128)(2,1)S(1)}, bf16[2,2,12,16,384]{4,3,2,1,0:T(8,128)(2,1)S(1)}, u32[]{:S(2)}, u32[]{:S(2)}) collective-permute-start(bf16[2,2,12,16,384]{4,3,2,1,0:T(8,128)(2,1)S(1)} %get-tuple-element.31), channel_id=1, source_target_pairs={{0,4},{1,5},{2,6},{3,7},{4,8},{5,9},{6,10},{7,11},{8,12},{9,13},{1... | collective-permute-start | bytes 1769480 | tf_op jit(solution)/shard_map/ppermute | solution.py:355
  100.8 53.6 %collective-permute-start.8 = (bf16[2,2,12,16,384]{4,3,2,1,0:T(8,128)(2,1)S(1)}, bf16[2,2,12,16,384]{4,3,2,1,0:T(8,128)(2,1)S(1)}, u32[]{:S(2)}, u32[]{:S(2)}) collective-permute-start(bf16[2,2,12,16,384]{4,3,2,1,0:T(8,128)(2,1)S(1)} %get-tuple-element.32), channel_id=1, source_target_pairs={{0,28},{1,29},{2,30},{3,31},{4,0},{5,1},{6,2},{7,3},{8,4},{9,5},{1... | collective-permute-start | bytes 1769480 | tf_op jit(solution)/shard_map/ppermute | solution.py:355
  107.0 26.9 %collective-permute-start.12 = (bf16[3,2,2,48,384]{4,3,2,1,0:T(8,128)(2,1)S(1)}, bf16[3,2,2,48,384]{4,3,2,1,0:T(8,128)(2,1)S(1)}, u32[]{:S(2)}, u32[]{:S(2)}) collective-permute-start(bf16[3,2,2,48,384]{4,3,2,1,0:T(8,128)(2,1)S(1)} %get-tuple-element.36), channel_id=1, source_target_pairs={{0,1},{1,0},{2,3},{3,2},{4,5},{5,4},{6,7},{7,6},{8,9},{9,8},{10,11... | collective-permute-start | bytes 1327112 | tf_op jit(solution)/shard_map/ppermute | solution.py:358
  126.7 12.7 %collective-permute-start.13 = (bf16[3,2,2,48,384]{4,3,2,1,0:T(8,128)(2,1)S(1)}, bf16[3,2,2,48,384]{4,3,2,1,0:T(8,128)(2,1)S(1)}, u32[]{:S(2)}, u32[]{:S(2)}) collective-permute-start(bf16[3,2,2,48,384]{4,3,2,1,0:T(8,128)(2,1)S(1)} %get-tuple-element.37), channel_id=1, source_target_pairs={{0,2},{1,3},{2,0},{3,1},{4,6},{5,7},{6,4},{7,5},{8,10},{9,11},{10,... | collective-permute-start | bytes 1327112 | tf_op jit(solution)/shard_map/ppermute | solution.py:358
  129.4 20.2 %collective-permute-start.14 = (bf16[3,2,2,48,384]{4,3,2,1,0:T(8,128)(2,1)S(1)}, bf16[3,2,2,48,384]{4,3,2,1,0:T(8,128)(2,1)S(1)}, u32[]{:S(2)}, u32[]{:S(2)}) collective-permute-start(bf16[3,2,2,48,384]{4,3,2,1,0:T(8,128)(2,1)S(1)} %get-tuple-element.38), channel_id=1, source_target_pairs={{0,3},{1,2},{2,1},{3,0},{4,7},{5,6},{6,5},{7,4},{8,11},{9,10},{10,... | collective-permute-start | bytes 1327112 | tf_op jit(solution)/shard_map/ppermute | solution.py:358
